TPU v7x, 8 devices: a whole 2x2x1 slice. The times are simulated.
8 devices in a mesh: part: 1 (over z), col: 2 (over y), row: 4 (over x, core).
Axes of the slice: x: 2, y: 2, z: 1, core: 2. Of those that a mesh axis runs over, the one named last changes fastest.
Arguments:
- mat_one: float32 [40, 128, 5120], P(('part', 'row'), None, 'col')
- mat_two: float32 [40, 128, 5120], P(('part', 'row'), None, 'col')
Outputs:
- output 1: float32 [40, 128, 5120], P(('part', 'row'), None, 'col')
- output 2: float32 [40, 128, 5120], P(('part', 'row'), None, 'col')
All inputs are finite; a program needn't handle non-finite values.
Results may differ from a plain program's by a relative error of at most 0.001.
Values sent between devices are 32-bit elements.
A program may use at most 1 GiB of HBM per device.

v0:
```python
import jax
import jax.numpy as jnp
from jax import lax
from jax.sharding import PartitionSpec as P

PRECISE = lax.Precision.HIGHEST


def factor_pair(local_mats, rows_n, cols_n):
    row_blocks, block_len, local_width = local_mats[0].shape
    col_blocks = local_width // block_len
    blocks = row_blocks * rows_n
    widest = max(rows_n, cols_n)
    my_row = lax.axis_index("row")
    my_col = lax.axis_index("col")
    row_ids = jnp.arange(row_blocks) * rows_n + my_row
    col_ids = jnp.arange(col_blocks) * cols_n + my_col
    identity = jnp.eye(block_len, dtype=jnp.float32)
    works = [local_mat.reshape(row_blocks * block_len, local_width) for local_mat in local_mats]
    for step_idx in range(blocks):
        own_row = step_idx % rows_n
        own_col = step_idx % cols_n
        diag_row = (step_idx // rows_n) * block_len
        diag_col = (step_idx // cols_n) * block_len
        base_block = (step_idx // widest) * widest
        row_lo = base_block // rows_n
        col_lo = base_block // cols_n
        in_col = my_col == own_col
        is_owner = jnp.logical_and(my_row == own_row, in_col)
        strip_ids = row_ids[row_lo:][:, None, None]
        below_diag = strip_ids > step_idx
        for mat_index in range(len(works)):
            work_mat = works[mat_index]
            diag_block = work_mat[diag_row:diag_row + block_len, diag_col:diag_col + block_len]
            diag_fac = jnp.linalg.cholesky(jnp.where(is_owner, diag_block, identity))
            diag_fac = lax.psum(jnp.where(my_row == own_row, diag_fac, 0.0), "row")
            col_strip = work_mat[row_lo * block_len:, diag_col:diag_col + block_len]
            solved = lax.linalg.triangular_solve(diag_fac, col_strip, left_side=False, lower=True, transpose_a=True)
            solved = solved.reshape(-1, block_len, block_len)
            old_strip = col_strip.reshape(-1, block_len, block_len)
            new_strip = jnp.where(below_diag, solved, jnp.where(strip_ids == step_idx, diag_fac, old_strip))
            new_strip = jnp.where(in_col, new_strip, old_strip)
            work_mat = lax.dynamic_update_slice(work_mat, new_strip.reshape(-1, block_len), (row_lo * block_len, diag_col))
            row_panel = lax.psum(jnp.where(jnp.logical_and(below_diag, in_col), solved, 0.0), "col")
            gathered = lax.all_gather(row_panel, "row")
            ordered = gathered.transpose(1, 0, 2, 3).reshape(-1, cols_n, block_len, block_len)
            col_panel = lax.dynamic_index_in_dim(ordered, my_col, axis=1, keepdims=False)
            trail_blk = work_mat[row_lo * block_len:, col_lo * block_len:]
            update = jnp.einsum("aub,cvb->aucv", row_panel, col_panel, precision=PRECISE, preferred_element_type=jnp.float32)
            work_mat = lax.dynamic_update_slice(work_mat, trail_blk - update.reshape(trail_blk.shape), (row_lo * block_len, col_lo * block_len))
            works[mat_index] = work_mat
    row_pos = (row_ids[:, None] * block_len + jnp.arange(block_len)[None, :]).reshape(-1, 1)
    col_pos = (col_ids[:, None] * block_len + jnp.arange(block_len)[None, :]).reshape(1, -1)
    lower_mask = row_pos >= col_pos
    return tuple(jnp.where(lower_mask, work_mat, 0.0).reshape(row_blocks, block_len, local_width) for work_mat in works)


def solution(mesh):
    rows_n = mesh.shape["row"]
    cols_n = mesh.shape["col"]
    block_spec = P(("part", "row"), None, "col")

    def run_pair(mat_one, mat_two):
        return factor_pair([mat_one, mat_two], rows_n, cols_n)

    return jax.shard_map(run_pair, mesh=mesh, in_specs=(block_spec, block_spec), out_specs=(block_spec, block_spec), check_vma=False)
```

profile of v0, /device:TPU:0, one launch (start us, length us, event | category | flops | bytes accessed | tf_op | source)
XLA Modules:
  0.0 6473.4 jit_solution(16176619155502495025)
XLA Ops:
  59.6 28.9 all-reduce.239.cloned.1.call-done
  115.3 40.1 all-reduce.319.cloned.1.call-done
  327.4 40.1 all-reduce.317.cloned.1.call-done
  485.4 26.1 all-reduce.235.cloned.1.call-done
  538.4 40.1 all-reduce.315.cloned.1.call-done
  696.2 26.1 all-reduce.233.cloned.1.call-done
  749.2 40.1 all-reduce.313.cloned.1.call-done
  903.8 26.3 all-reduce.231.cloned.1.call-done
  956.6 37.2 all-reduce.311.cloned.1.call-done
  1102.3 26.1 all-reduce.229.cloned.1.call-done
  1154.9 37.2 all-reduce.309.cloned.1.call-done
  1300.2 26.2 all-reduce.227.cloned.1.call-done
  1353.0 37.2 all-reduce.307.cloned.1.call-done
  1498.4 26.2 all-reduce.225.cloned.1.call-done
  1551.9 37.2 all-reduce.305.cloned.1.call-done
  1697.4 26.0 all-reduce.223.cloned.1.call-done
  1749.7 34.4 all-reduce.303.cloned.1.call-done
  1887.1 26.2 all-reduce.221.cloned.1.call-done
  1939.5 34.4 all-reduce.301.cloned.1.call-done
  2076.9 26.2 all-reduce.219.cloned.1.call-done
  2129.3 34.4 all-reduce.299.cloned.1.call-done
  2266.5 26.3 all-reduce.217.cloned.1.call-done
  2318.9 34.4 all-reduce.297.cloned.1.call-done
  2456.1 26.3 all-reduce.215.cloned.1.call-done
  2508.4 31.5 all-reduce.295.cloned.1.call-done
  2634.8 26.3 all-reduce.213.cloned.1.call-done
  2687.0 31.5 all-reduce.293.cloned.1.call-done
  2813.2 26.3 all-reduce.211.cloned.1.call-done
  2865.5 31.5 all-reduce.291.cloned.1.call-done
  2991.8 26.3 all-reduce.209.cloned.1.call-done
  3044.0 31.5 all-reduce.289.cloned.1.call-done
  3170.3 26.3 all-reduce.207.cloned.1.call-done
  3222.1 28.7 all-reduce.287.cloned.1.call-done
  3337.9 25.9 all-reduce.205.cloned.1.call-done
  3389.6 28.7 all-reduce.285.cloned.1.call-done
  3505.0 26.1 all-reduce.203.cloned.1.call-done
  3557.1 28.7 all-reduce.283.cloned.1.call-done
  3672.9 26.1 all-reduce.201.cloned.1.call-done
  3725.0 28.7 all-reduce.281.cloned.1.call-done
  3840.7 25.9 all-reduce.199.cloned.1.call-done
  3994.6 26.2 all-reduce.197.cloned.1.call-done
  4148.7 26.3 all-reduce.195.cloned.1.call-done
  4302.7 26.3 all-reduce.193.cloned.1.call-done
  4456.6 26.3 all-reduce.191.cloned.1.call-done
  4602.1 26.2 all-reduce.189.cloned.1.call-done
  4748.1 25.9 all-reduce.187.cloned.1.call-done
  4893.6 26.1 all-reduce.185.cloned.1.call-done
  5166.3 25.9 all-reduce.181.cloned.1.call-done
  (1959 shorter events, 5023.2 us)
Async XLA Ops:
  59.2 96.2 %all-reduce.319.cloned.1.call-start = ((), (), s32[]{:S(2)}) async-start(), calls=%async_computation.135 | async-start | bytes 2621440 | tf_op jit(solution)/shard_map/psum | solution.py:44
  156.0 144.6 %all-reduce.237.cloned.1.call-start = ((), (), s32[]{:S(2)}) async-start(), calls=%async_computation.94 | async-start | bytes 262144 | tf_op jit(solution)/shard_map/psum | solution.py:36
  274.2 93.3 %all-reduce.317.cloned.1.call-start = ((), (), s32[]{:S(2)}) async-start(), calls=%async_computation.134 | async-start | bytes 2621440 | tf_op jit(solution)/shard_map/psum | solution.py:44
  368.3 143.2 %all-reduce.235.cloned.1.call-start = ((), (), s32[]{:S(2)}) async-start(), calls=%async_computation.93 | async-start | bytes 262144 | tf_op jit(solution)/shard_map/psum | solution.py:36
  485.1 93.4 %all-reduce.315.cloned.1.call-start = ((), (), s32[]{:S(2)}) async-start(), calls=%async_computation.133 | async-start | bytes 2621440 | tf_op jit(solution)/shard_map/psum | solution.py:44
  579.1 143.2 %all-reduce.233.cloned.1.call-start = ((), (), s32[]{:S(2)}) async-start(), calls=%async_computation.92 | async-start | bytes 262144 | tf_op jit(solution)/shard_map/psum | solution.py:36
  695.9 93.3 %all-reduce.313.cloned.1.call-start = ((), (), s32[]{:S(2)}) async-start(), calls=%async_computation.132 | async-start | bytes 2621440 | tf_op jit(solution)/shard_map/psum | solution.py:44
  789.8 140.2 %all-reduce.231.cloned.1.call-start = ((), (), s32[]{:S(2)}) async-start(), calls=%async_computation.91 | async-start | bytes 262144 | tf_op jit(solution)/shard_map/psum | solution.py:36
  903.7 90.1 %all-reduce.311.cloned.1.call-start = ((), (), s32[]{:S(2)}) async-start(), calls=%async_computation.131 | async-start | bytes 2359296 | tf_op jit(solution)/shard_map/psum | solution.py:44
  994.4 134.0 %all-reduce.229.cloned.1.call-start = ((), (), s32[]{:S(2)}) async-start(), calls=%async_computation.90 | async-start | bytes 262144 | tf_op jit(solution)/shard_map/psum | solution.py:36
  1102.0 90.2 %all-reduce.309.cloned.1.call-start = ((), (), s32[]{:S(2)}) async-start(), calls=%async_computation.130 | async-start | bytes 2359296 | tf_op jit(solution)/shard_map/psum | solution.py:44
  1192.7 133.8 %all-reduce.227.cloned.1.call-start = ((), (), s32[]{:S(2)}) async-start(), calls=%async_computation.89 | async-start | bytes 262144 | tf_op jit(solution)/shard_map/psum | solution.py:36
  1300.1 90.1 %all-reduce.307.cloned.1.call-start = ((), (), s32[]{:S(2)}) async-start(), calls=%async_computation.129 | async-start | bytes 2359296 | tf_op jit(solution)/shard_map/psum | solution.py:44
  1391.0 133.7 %all-reduce.225.cloned.1.call-start = ((), (), s32[]{:S(2)}) async-start(), calls=%async_computation.88 | async-start | bytes 262144 | tf_op jit(solution)/shard_map/psum | solution.py:36
  1498.2 90.9 %all-reduce.305.cloned.1.call-start = ((), (), s32[]{:S(2)}) async-start(), calls=%async_computation.128 | async-start | bytes 2359296 | tf_op jit(solution)/shard_map/psum | solution.py:44
  1589.9 133.5 %all-reduce.223.cloned.1.call-start = ((), (), s32[]{:S(2)}) async-start(), calls=%async_computation.87 | async-start | bytes 262144 | tf_op jit(solution)/shard_map/psum | solution.py:36
  1697.0 87.0 %all-reduce.303.cloned.1.call-start = ((), (), s32[]{:S(2)}) async-start(), calls=%async_computation.127 | async-start | bytes 2097152 | tf_op jit(solution)/shard_map/psum | solution.py:44
  1784.7 128.6 %all-reduce.221.cloned.1.call-start = ((), (), s32[]{:S(2)}) async-start(), calls=%async_computation.86 | async-start | bytes 262144 | tf_op jit(solution)/shard_map/psum | solution.py:36
  1974.7 128.5 %all-reduce.219.cloned.1.call-start = ((), (), s32[]{:S(2)}) async-start(), calls=%async_computation.85 | async-start | bytes 262144 | tf_op jit(solution)/shard_map/psum | solution.py:36
  2164.5 128.3 %all-reduce.217.cloned.1.call-start = ((), (), s32[]{:S(2)}) async-start(), calls=%async_computation.84 | async-start | bytes 262144 | tf_op jit(solution)/shard_map/psum | solution.py:36
  2353.9 128.5 %all-reduce.215.cloned.1.call-start = ((), (), s32[]{:S(2)}) async-start(), calls=%async_computation.83 | async-start | bytes 262144 | tf_op jit(solution)/shard_map/psum | solution.py:36
  2540.7 120.4 %all-reduce.213.cloned.1.call-start = ((), (), s32[]{:S(2)}) async-start(), calls=%async_computation.82 | async-start | bytes 262144 | tf_op jit(solution)/shard_map/psum | solution.py:36
  2719.3 120.3 %all-reduce.211.cloned.1.call-start = ((), (), s32[]{:S(2)}) async-start(), calls=%async_computation.81 | async-start | bytes 262144 | tf_op jit(solution)/shard_map/psum | solution.py:36
  2897.8 120.3 %all-reduce.209.cloned.1.call-start = ((), (), s32[]{:S(2)}) async-start(), calls=%async_computation.80 | async-start | bytes 262144 | tf_op jit(solution)/shard_map/psum | solution.py:36
  3076.2 120.4 %all-reduce.207.cloned.1.call-start = ((), (), s32[]{:S(2)}) async-start(), calls=%async_computation.79 | async-start | bytes 262144 | tf_op jit(solution)/shard_map/psum | solution.py:36
  3251.6 112.2 %all-reduce.205.cloned.1.call-start = ((), (), s32[]{:S(2)}) async-start(), calls=%async_computation.78 | async-start | bytes 262144 | tf_op jit(solution)/shard_map/psum | solution.py:36
  3418.9 112.3 %all-reduce.203.cloned.1.call-start = ((), (), s32[]{:S(2)}) async-start(), calls=%async_computation.77 | async-start | bytes 262144 | tf_op jit(solution)/shard_map/psum | solution.py:36
  3586.4 112.6 %all-reduce.201.cloned.1.call-start = ((), (), s32[]{:S(2)}) async-start(), calls=%async_computation.76 | async-start | bytes 262144 | tf_op jit(solution)/shard_map/psum | solution.py:36
  3754.4 112.2 %all-reduce.199.cloned.1.call-start = ((), (), s32[]{:S(2)}) async-start(), calls=%async_computation.75 | async-start | bytes 262144 | tf_op jit(solution)/shard_map/psum | solution.py:36
  3918.6 102.2 %all-reduce.197.cloned.1.call-start = ((), (), s32[]{:S(2)}) async-start(), calls=%async_computation.74 | async-start | bytes 262144 | tf_op jit(solution)/shard_map/psum | solution.py:36
  4072.6 102.4 %all-reduce.195.cloned.1.call-start = ((), (), s32[]{:S(2)}) async-start(), calls=%async_computation.73 | async-start | bytes 262144 | tf_op jit(solution)/shard_map/psum | solution.py:36
  4226.6 102.4 %all-reduce.193.cloned.1.call-start = ((), (), s32[]{:S(2)}) async-start(), calls=%async_computation.72 | async-start | bytes 262144 | tf_op jit(solution)/shard_map/psum | solution.py:36
  4380.9 102.0 %all-reduce.191.cloned.1.call-start = ((), (), s32[]{:S(2)}) async-start(), calls=%async_computation.71 | async-start | bytes 262144 | tf_op jit(solution)/shard_map/psum | solution.py:36
  4531.4 97.0 %all-reduce.189.cloned.1.call-start = ((), (), s32[]{:S(2)}) async-start(), calls=%async_computation.70 | async-start | bytes 262144 | tf_op jit(solution)/shard_map/psum | solution.py:36
  4676.9 97.1 %all-reduce.187.cloned.1.call-start = ((), (), s32[]{:S(2)}) async-start(), calls=%async_computation.69 | async-start | bytes 262144 | tf_op jit(solution)/shard_map/psum | solution.py:36
  4822.6 97.1 %all-reduce.185.cloned.1.call-start = ((), (), s32[]{:S(2)}) async-start(), calls=%async_computation.68 | async-start | bytes 262144 | tf_op jit(solution)/shard_map/psum | solution.py:36
  4968.4 97.2 %all-reduce.183.cloned.1.call-start = ((), (), s32[]{:S(2)}) async-start(), calls=%async_computation.67 | async-start | bytes 262144 | tf_op jit(solution)/shard_map/psum | solution.py:36
  5090.3 101.9 %all-reduce.181.cloned.1.call-start = ((), (), s32[]{:S(2)}) async-start(), calls=%async_computation.66 | async-start | bytes 262144 | tf_op jit(solution)/shard_map/psum | solution.py:36
  5215.9 101.9 %all-reduce.179.cloned.1.call-start = ((), (), s32[]{:S(2)}) async-start(), calls=%async_computation.65 | async-start | bytes 262144 | tf_op jit(solution)/shard_map/psum | solution.py:36
  5341.5 101.8 %all-reduce.177.cloned.1.call-start = ((), (), s32[]{:S(2)}) async-start(), calls=%async_computation.64 | async-start | bytes 262144 | tf_op jit(solution)/shard_map/psum | solution.py:36
  5467.1 101.9 %all-reduce.175.cloned.1.call-start = ((), (), s32[]{:S(2)}) async-start(), calls=%async_computation.63 | async-start | bytes 262144 | tf_op jit(solution)/shard_map/psum | solution.py:36
  5592.5 95.0 %all-reduce.173.cloned.1.call-start = ((), (), s32[]{:S(2)}) async-start(), calls=%async_computation.62 | async-start | bytes 262144 | tf_op jit(solution)/shard_map/psum | solution.py:36
  5711.0 95.0 %all-reduce.171.cloned.1.call-start = ((), (), s32[]{:S(2)}) async-start(), calls=%async_computation.61 | async-start | bytes 262144 | tf_op jit(solution)/shard_map/psum | solution.py:36
  5829.6 94.9 %all-reduce.169.cloned.1.call-start = ((), (), s32[]{:S(2)}) async-start(), calls=%async_computation.60 | async-start | bytes 262144 | tf_op jit(solution)/shard_map/psum | solution.py:36
  5948.1 95.6 %all-reduce.167.cloned.1.call-start = ((), (), s32[]{:S(2)}) async-start(), calls=%async_computation.59 | async-start | bytes 262144 | tf_op jit(solution)/shard_map/psum | solution.py:36
  6068.5 90.7 %all-reduce.165.cloned.1.call-start = ((), (), s32[]{:S(2)}) async-start(), calls=%async_computation.58 | async-start | bytes 262144 | tf_op jit(solution)/shard_map/psum | solution.py:36
  6182.3 90.8 %all-reduce.163.cloned.1.call-start = ((), (), s32[]{:S(2)}) async-start(), calls=%async_computation.57 | async-start | bytes 262144 | tf_op jit(solution)/shard_map/psum | solution.py:36
  6296.3 92.4 %all-reduce.161.cloned.1.call-start = ((), (), s32[]{:S(2)}) async-start(), calls=%async_computation.56 | async-start | bytes 262144 | tf_op jit(solution)/shard_map/psum | solution.py:36
  (214 other events, 7746.4 us)
Sparse Core Ops, SparseCore 0:
  59.3 29.0 all-reduce.238
  115.4 39.9 all-reduce.318
  274.3 26.2 all-reduce.236
  327.5 39.9 all-reduce.316
  485.2 26.2 all-reduce.234
  538.5 39.9 all-reduce.314
  696.0 26.2 all-reduce.232
  749.2 39.9 all-reduce.312
  903.8 26.2 all-reduce.230
  956.6 37.1 all-reduce.310
  1102.1 26.2 all-reduce.228
  1154.9 37.1 all-reduce.308
  1300.2 26.2 all-reduce.226
  1353.0 37.1 all-reduce.306
  1498.4 26.2 all-reduce.224
  1552.0 37.1 all-reduce.304
  1697.1 26.2 all-reduce.222
  1749.8 34.2 all-reduce.302
  1887.1 26.2 all-reduce.220
  1939.6 34.2 all-reduce.300
  2076.9 26.2 all-reduce.218
  2129.4 34.2 all-reduce.298
  2266.5 26.2 all-reduce.216
  2319.0 34.2 all-reduce.296
  2456.1 26.2 all-reduce.214
  2508.5 31.4 all-reduce.294
  2634.8 26.2 all-reduce.212
  2687.0 31.4 all-reduce.292
  2813.2 26.2 all-reduce.210
  2865.5 31.4 all-reduce.290
  2991.8 26.2 all-reduce.208
  3044.1 31.4 all-reduce.288
  3170.3 26.2 all-reduce.206
  3222.2 28.5 all-reduce.286
  3337.5 26.2 all-reduce.204
  3389.7 28.5 all-reduce.284
  3504.8 26.2 all-reduce.202
  3557.2 28.5 all-reduce.282
  3672.7 26.2 all-reduce.200
  3725.0 28.5 all-reduce.280
  3840.3 26.2 all-reduce.198
  4148.7 26.2 all-reduce.194
  4302.7 26.2 all-reduce.192
  4456.6 26.2 all-reduce.190
  4602.1 26.2 all-reduce.188
  4747.6 26.2 all-reduce.186
  4893.4 26.2 all-reduce.184
  5039.3 26.2 all-reduce.182
  (88 shorter events, 1727.3 us)
where the time goes:
time: 6500 us; the launch traced here: 6470 us
  waiting for transfers between devices  3010 us (46%)
  other arithmetic  2060 us (32%)
  matrix products  674 us (10%)
  local copies, waits for them, and re-layouts  452 us (7%)
  blocking collectives  238 us (4%)
    psum x40, waiting for transfers between devices, factor_pair(): lax.psum(jnp.where(jnp.logical_and(below_diag, in_col), solved, 0.0), 'col')  1070 us
    psum x40, waiting for transfers between devices, factor_pair(): diag_fac = lax.psum(jnp.where(my_row == own_row, diag_fac, 0.0), 'row')  1040 us
    another operation x240, other arithmetic, factor_pair(): diag_fac = jnp.linalg.cholesky(jnp.where(is_owner, diag_block, identity))  997 us
    all_gather x56, waiting for transfers between devices, factor_pair(): gathered = lax.all_gather(row_panel, 'row')  882 us
    another operation x160, other arithmetic, factor_pair(): lax.linalg.triangular_solve(diag_fac, col_strip, left_side=False, lower=T...  853 us
    dot_general x80, matrix products, factor_pair(): jnp.einsum('aub,cvb->aucv', row_panel, col_panel, precision=PRECISE, pref...  555 us
    all_gather x24, blocking collectives, factor_pair(): gathered = lax.all_gather(row_panel, 'row')  238 us
    unnamed x254, local copies, waits for them, and re-layouts  166 us
  transfers between devices with their start and end apart: 136, of which 136 were waited for; matrix products, arithmetic and copies ran while one was open for 3% of the time, Pallas kernels for 0%

commit v1 on v0

v1 whole, which is shorter than its diff:
```python
import functools

import jax
import jax.numpy as jnp
from jax import lax
from jax.experimental import pallas as pl
from jax.experimental.pallas import tpu as pltpu
from jax.sharding import PartitionSpec as P

PRECISE = lax.Precision.HIGHEST
NB = 128
VMEM_SPEC = pl.BlockSpec(memory_space=pltpu.VMEM)
HBM_SPEC = pl.BlockSpec(memory_space=pltpu.HBM)
SMEM_SPEC = pl.BlockSpec(memory_space=pltpu.SMEM)
LIMIT = 60 * 1024 * 1024


def nt(a, b):
    return lax.dot_general(a, b, (((1,), (1,)), ((), ())), precision=PRECISE, preferred_element_type=jnp.float32)


def factor_128(block):
    lane = lax.broadcasted_iota(jnp.int32, (8, 128), 1)
    sub = lax.broadcasted_iota(jnp.int32, (8, 128), 0)
    wide = (8, 128)
    rows = [block[8 * q:8 * q + 8, :] for q in range(16)]
    done, diag_parts = [], []
    for p in range(16):
        cur = rows[p]
        lo = 8 * p
        inside = jnp.logical_and(lane >= lo, lane < lo + 8)
        cols = [jnp.broadcast_to(cur[:, lo + j:lo + j + 1], wide) for j in range(8)]
        has_next = p < 15
        if has_next:
            nxt = rows[p + 1]
            ncols = [jnp.broadcast_to(nxt[:, lo + j:lo + j + 1], wide) for j in range(8)]
            nxt = jnp.where(inside, 0.0, nxt)
        cur = jnp.where(inside, jnp.where(lane - lo == sub, 1.0, 0.0), cur)
        diag_part = jnp.zeros(wide, jnp.float32)
        for j in range(8):
            pivot = jnp.broadcast_to(cols[j][j:j + 1, :], wide)
            inv_root = lax.rsqrt(pivot)
            lcol = cols[j] * inv_root
            for m in range(j + 1, 8):
                cols[m] = cols[m] - lcol * jnp.broadcast_to(lcol[m:m + 1, :], wide)
            wrow = jnp.broadcast_to(cur[j:j + 1, :], wide) * inv_root
            cur = jnp.where(sub == j, wrow, cur - jnp.where(sub > j, lcol, 0.0) * wrow)
            if has_next:
                ncol = ncols[j] * inv_root
                nxt = nxt - ncol * wrow
                for m in range(j + 1, 8):
                    ncols[m] = ncols[m] - ncol * jnp.broadcast_to(lcol[m:m + 1, :], wide)
            diag_part = jnp.where(jnp.logical_and(lane == lo + j, sub >= j), lcol, diag_part)
        done.append(cur)
        diag_parts.append(diag_part)
        if has_next:
            rows[p + 1] = nxt
        if p < 14:
            flipped = cur.T
            for q in range(p + 2, 16):
                acc = jnp.where(inside, 0.0, rows[q])
                for j in range(8):
                    acc = acc - jnp.broadcast_to(flipped[8 * q:8 * q + 8, j:j + 1], wide) * jnp.broadcast_to(cur[j:j + 1, :], wide)
                rows[q] = acc
    packed = jnp.concatenate(done, axis=0)
    diag8 = jnp.concatenate(diag_parts, axis=0)
    full_lane = lax.broadcasted_iota(jnp.int32, (128, 128), 1) // 8
    full_sub = lax.broadcasted_iota(jnp.int32, (128, 128), 0) // 8
    inverse = jnp.where(full_lane <= full_sub, packed, 0.0)
    upper = jnp.where(full_lane > full_sub, packed, 0.0)
    return upper.T + diag8, inverse

def chain_kernel(s_ref, l_ref, inv_ref, work):
    work[...] = s_ref[...]
    n = s_ref.shape[0] // 128
    rowb = lax.broadcasted_iota(jnp.int32, (n * 128, 128), 0) // 128
    def step(k, _):
        lo = pl.multiple_of(k * 128, 128)
        fac, inv = factor_128(work[pl.ds(lo, 128), pl.ds(lo, 128)])
        inv_ref[pl.ds(lo, 128), :] = inv
        col = nt(work[:, pl.ds(lo, 128)], inv)
        col = jnp.where(rowb > k, col, 0.0)
        l_ref[:, pl.ds(lo, 128)] = col
        l_ref[pl.ds(lo, 128), pl.ds(lo, 128)] = fac
        work[...] = work[...] - nt(col, col)
        return 0
    lax.fori_loop(0, n, step, 0)


def shape_of(*dims):
    return jax.ShapeDtypeStruct(dims, jnp.float32)


def cost(flops):
    return pl.CostEstimate(flops=int(flops), bytes_accessed=1 << 20, transcendentals=0)


def chain(s):
    n = s.shape[0]
    return pl.pallas_call(
        chain_kernel,
        out_shape=(shape_of(n, n), shape_of(n, NB)),
        in_specs=[VMEM_SPEC],
        out_specs=(VMEM_SPEC,) * 2,
        scratch_shapes=[pltpu.VMEM((n, n), jnp.float32)],
        cost_estimate=cost(2.5e9),
        name="chain",
    )(s)


def solve_kernel(rows_n, rest, ahead, *refs):
    me_ref, lss_ref, inv_ref = refs[:3]
    sub_refs = refs[3:3 + rows_n]
    next_refs = refs[3 + rows_n:3 + 2 * rows_n]
    pos = 3 + 2 * rows_n
    if ahead:
        own_ref, w_ref, lown_ref, sb_ref, wout_ref, panel = refs[pos:]
    else:
        lown_ref, sb_ref, panel = refs[pos:]
    me = me_ref[0]
    wide = rows_n * NB
    for k in range(rows_n):
        lo = pl.multiple_of(lax.bitwise_xor(me, k) * NB, NB)
        panel[pl.ds(lo, NB), :] = sub_refs[k][...]
        sb_ref[pl.ds(lo, NB), :] = next_refs[k][...]
    if ahead:
        panel[wide:, :] = own_ref[NB:, :]
    for k in range(rows_n):
        cols = slice(k * NB, (k + 1) * NB)
        solved = nt(panel[:, cols], inv_ref[cols, :])
        panel[:, cols] = solved
        if k + 1 < rows_n:
            panel[:, (k + 1) * NB:] = panel[:, (k + 1) * NB:] - nt(solved, lss_ref[(k + 1) * NB:, cols])
    sub = panel[:wide, :]
    sb_ref[...] = sb_ref[...] - nt(sub, sub)
    lown_ref[:NB, :] = panel[pl.ds(pl.multiple_of(me * NB, NB), NB), :]
    if ahead:
        lown_ref[NB:, :] = panel[wide:, :]
        wout_ref[...] = w_ref[...] - nt(panel[wide:, :], sub)


def solve(me, lss, inv, own, sub_rel, next_rel, w_rest):
    rows_n = len(sub_rel)
    wide = rows_n * NB
    rest = w_rest.shape[0] if w_rest is not None else 0
    ahead = rest > 0
    args = [me, lss, inv, *sub_rel, *next_rel]
    outs = [shape_of(NB + rest, wide), shape_of(wide, wide)]
    if ahead:
        args += [own, w_rest]
        outs.append(shape_of(rest, wide))
    return pl.pallas_call(
        functools.partial(solve_kernel, rows_n, rest, ahead),
        out_shape=tuple(outs),
        in_specs=[SMEM_SPEC] + [VMEM_SPEC] * (len(args) - 1),
        out_specs=(VMEM_SPEC,) * len(outs),
        scratch_shapes=[pltpu.VMEM((wide + rest, wide), jnp.float32)],
        compiler_params=pltpu.CompilerParams(vmem_limit_bytes=LIMIT),
        cost_estimate=cost(2 * (wide + rest) * wide * wide * 2),
        name="solve",
    )(*args)


def update_kernel(rows_n, terms, height, *refs):
    me_ref, w_ref = refs[:2]
    count = len(terms)
    left_refs = refs[2:2 + count]
    right_refs = refs[2 + count:2 + count + count * rows_n]
    out_ref, left, right, sem = refs[2 + count + count * rows_n:]
    me = me_ref[0]
    wide = rows_n * NB
    pending = []
    for i, (left_lo, right_los) in enumerate(terms):
        copies = [pltpu.make_async_copy(left_refs[i].at[pl.ds(left_lo, height), :], left.at[i], sem.at[i, rows_n])]
        for k in range(rows_n):
            lo = pl.multiple_of(lax.bitwise_xor(me, k) * NB, NB)
            copies.append(pltpu.make_async_copy(
                right_refs[i * rows_n + k].at[pl.ds(right_los[k], NB), :], right.at[i, pl.ds(lo, NB), :], sem.at[i, k]))
        for copy in copies:
            copy.start()
        pending.append(copies)
    out_ref[...] = w_ref[...]
    for i in range(count):
        for copy in pending[i]:
            copy.wait()
        out_ref[...] = out_ref[...] - nt(left[i], right[i])


def update(me, w, lefts, rights, terms):
    rows_n = len(rights[0])
    wide = rows_n * NB
    height = w.shape[0]
    count = len(terms)
    args = [me, w, *lefts, *[piece for group in rights for piece in group]]
    return pl.pallas_call(
        functools.partial(update_kernel, rows_n, terms, height),
        out_shape=shape_of(height, wide),
        in_specs=[SMEM_SPEC, VMEM_SPEC] + [HBM_SPEC] * (len(args) - 2),
        out_specs=VMEM_SPEC,
        scratch_shapes=[
            pltpu.VMEM((count, height, wide), jnp.float32),
            pltpu.VMEM((count, wide, wide), jnp.float32),
            pltpu.SemaphoreType.DMA((count, rows_n + 1)),
        ],
        compiler_params=pltpu.CompilerParams(vmem_limit_bytes=LIMIT),
        cost_estimate=cost(2 * height * wide * wide * count * 2),
        name="update",
    )(*args)


def tie(first, second):
    return lax.optimization_barrier((first, second))


def factor_pair(mat_one, mat_two, rows_n, cols_n):
    row_blocks, block_len, local_width = mat_one.shape
    steps = row_blocks
    wide = rows_n * NB
    half = wide // cols_n
    per = half // NB
    my_row = lax.axis_index("row")
    first = lax.axis_index("col") == 0
    me = my_row.astype(jnp.int32).reshape(1)
    swap = [(0, 1), (1, 0)]

    def hop(value, mask):
        return lax.ppermute(value, "row", [(i, i ^ mask) for i in range(rows_n)])

    def gather(value):
        far = hop(value, 2)
        return [value, hop(value, 1), far, hop(far, 1)]

    def panel_of(step, row_lo, row_hi):
        cols = slice(step * half, (step + 1) * half)
        piece_one, piece_two = mat_one[row_lo:row_hi, :, cols], mat_two[row_lo:row_hi, :, cols]
        mine = jnp.where(first, piece_one, piece_two)
        got = lax.ppermute(jnp.where(first, piece_two, piece_one), "col", swap)
        even, odd = jnp.where(first, mine, got), jnp.where(first, got, mine)
        parts = []
        for q in range(per):
            parts += [even[..., q * NB:(q + 1) * NB], odd[..., q * NB:(q + 1) * NB]]
        return jnp.concatenate(parts, axis=-1).reshape(-1, wide)

    def in_order(rel):
        picked = []
        for q in range(rows_n):
            value = rel[rows_n - 1]
            for k in range(rows_n - 1):
                value = jnp.where(my_row == (q ^ k), rel[k], value)
            picked.append(value)
        return jnp.concatenate(picked, axis=0)

    sb = in_order(gather(panel_of(0, 0, 1)))
    sub_own = panel_of(0, 1, 2)
    own = jnp.concatenate([sub_own, panel_of(0, 2, steps)], axis=0)
    sub_rel = gather(sub_own)
    diag_own = panel_of(1, 1, 2)
    rest_own = panel_of(1, 2, steps)
    raw = [None, None] + [panel_of(s, s, steps) for s in range(2, steps)]
    lowns, near, later = [], [], []
    out_one, out_two = [], []

    def emit(step, lss_rows, lown):
        full = lss_rows if lown is None else jnp.concatenate([lss_rows, lown], axis=0)
        full = full.reshape(-1, per, cols_n, NB)
        even, odd = full[:, :, 0], full[:, :, 1]
        kept = jnp.where(first, even, odd).reshape(-1, NB, half)
        got = lax.ppermute(jnp.where(first, odd, even).reshape(-1, NB, half), "col", swap)
        pads = ((step, 0), (0, 0), (0, 0))
        out_one.append(jnp.pad(jnp.where(first, kept, got), pads))
        out_two.append(jnp.pad(jnp.where(first, got, kept), pads))

    for step in range(steps):
        lss, inv = chain(sb)
        lss_rows = lax.dynamic_slice(lss, (my_row * NB, 0), (NB, wide))
        if step == steps - 1:
            emit(step, lss_rows, None)
            break
        target = step + 1
        if step >= 1:
            lefts, rights, terms_diag, terms_rest = [], [], [], []
            for past in range(step):
                base = (target - past - 1) * NB
                lefts.append(lowns[past])
                if past == step - 1:
                    rights.append([lowns[past]] + near[past][1:])
                    los = (base,) + (0,) * (rows_n - 1)
                else:
                    rights.append([lowns[past]] + later[past][1:])
                    los = (base,) + ((target - past - 3) * NB,) * (rows_n - 1)
                terms_diag.append((base, los))
                terms_rest.append((base + NB, los))
            panel = raw[target]
            lss, panel = tie(lss, panel)
            diag_own = update(me, panel[:NB], lefts, rights, terms_diag)
            rest_own = None
            if target < steps - 1:
                diag_own, rest_raw = tie(diag_own, panel[NB:])
                rest_own = update(me, rest_raw, lefts, rights, terms_rest)
        next_rel = gather(diag_own)
        if step == steps - 2:
            rest_own = None
        res = solve(me, lss, inv, own, sub_rel, next_rel, rest_own)
        lown, sb = res[0], res[1]
        lowns.append(lown)
        if rest_own is not None:
            own = res[2]
            sub_rel = gather(own[:NB])
        if step <= steps - 3:
            near.append(gather(lown[NB:2 * NB]))
        if step <= steps - 4:
            later.append(gather(lown[2 * NB:]))
        else:
            later.append(None)
        emit(step, lss_rows, lown)
    return jnp.concatenate(out_one, axis=-1), jnp.concatenate(out_two, axis=-1)


def solution(mesh):
    rows_n = mesh.shape["row"]
    cols_n = mesh.shape["col"]
    block_spec = P(("part", "row"), None, "col")

    def run_pair(mat_one, mat_two):
        return factor_pair(mat_one, mat_two, rows_n, cols_n)

    return jax.shard_map(run_pair, mesh=mesh, in_specs=(block_spec, block_spec), out_specs=(block_spec, block_spec), check_vma=False)
```

time: 6500 us -> 1040 us (0.16)
  waiting for transfers between devices: 3010 us -> 159 us
  other arithmetic: 2060 us -> 90.1 us
  matrix products: 674 us -> 0 us
  Pallas kernels: 0 us -> 527 us
  local copies, waits for them, and re-layouts: 452 us -> 182 us
  blocking collectives: 238 us -> 0 us
    psum x80 -> x0, waiting for transfers between devices: 2110 us -> none  [the longest x40 1070 us: factor_pair(): lax.psum(jnp.where(jnp.logical_and(below_diag, in_col), solved, 0.0), 'col')]
    another operation x400 -> x0, other arithmetic: 1850 us -> none  [the longest x240 997 us: factor_pair(): diag_fac = jnp.linalg.cholesky(jnp.where(is_owner, diag_block, identity))]
    all_gather x56 -> x0, waiting for transfers between devices: 882 us -> none  [factor_pair(): gathered = lax.all_gather(row_panel, 'row')]
    dot_general x80 -> x0, matrix products: 555 us -> none  [factor_pair(): jnp.einsum('aub,cvb->aucv', row_panel, col_panel, precision=PRECISE, pref...]
    pallas_call x0 -> x34, Pallas kernels: none -> 527 us  [the longest x10 255 us: chain(): pl.pallas_call(chain_kernel, out_shape=(shape_of(n, n), shape_of(n, NB)),...]
    all_gather x24 -> x0, blocking collectives: 238 us -> none  [factor_pair(): gathered = lax.all_gather(row_panel, 'row')]
    dynamic_update_slice x110 -> x0, local copies, waits for them, and re-layouts: 165 us -> none  [the longest x38 109 us: factor_pair(): lax.dynamic_update_slice(work_mat, trail_blk - update.reshape(trail_blk.s...]
    ppermute x0 -> x125, waiting for transfers between devices: none -> 159 us  [the longest x102 80.8 us: hop(): return lax.ppermute(value, 'row', [(i, i ^ mask) for i in range(rows_n)])]
  transfers between devices with their start and end apart: 136 -> 125, of which waited for: 136 -> 19; matrix products, arithmetic and copies ran while one was open for 3% -> 24% of each run, Pallas kernels for 0% -> 48%
where the time goes in v1:
time: 1040 us; the launch traced here: 1030 us
  Pallas kernels  527 us (51%)
  local copies, waits for them, and re-layouts  182 us (18%)
  waiting for transfers between devices  159 us (15%)
  other arithmetic  90.1 us (9%)
  starting transfers between devices  73.3 us (7%)
    pallas_call x10, Pallas kernels, chain(): pl.pallas_call(chain_kernel, out_shape=(shape_of(n, n), shape_of(n, NB)),...  255 us
    pallas_call x15, Pallas kernels, update(): pl.pallas_call(functools.partial(update_kernel, rows_n, terms, height), o...  139 us
    pallas_call x9, Pallas kernels, solve(): pl.pallas_call(functools.partial(solve_kernel, rows_n, rest, ahead), out_...  132 us
    ppermute x102, waiting for transfers between devices, hop(): return lax.ppermute(value, 'row', [(i, i ^ mask) for i in range(rows_n)])  80.8 us
    ppermute x13, waiting for transfers between devices, panel_of(): got = lax.ppermute(jnp.where(first, piece_two, piece_one), 'col', swap)  74.3 us
    ppermute x102, starting transfers between devices, hop(): return lax.ppermute(value, 'row', [(i, i ^ mask) for i in range(rows_n)])  47.2 us
    unnamed x176, local copies, waits for them, and re-layouts  34.9 us
    reshape x9, local copies, waits for them, and re-layouts, emit(): full = full.reshape(-1, per, cols_n, NB)  22.9 us
  transfers between devices with their start and end apart: 125, of which 19 were waited for; matrix products, arithmetic and copies ran while one was open for 24% of the time, Pallas kernels for 48%

profile of v1, /device:TPU:0, one launch (start us, length us, event | category | flops | bytes accessed | tf_op | source)
XLA Modules:
  0.0 1032.9 jit_solution(6858821011403229755)
XLA Ops:
  26.9 29.4 %collective-permute-done.8 = f32[1,128,256]{2,1,0:T(8,128)S(1)} collective-permute-done((f32[1,128,256]{2,1,0:T(8,128)S(1)}, f32[1,128,256]{2,1,0:T(8,128)S(1)}, u32[]{:S(2)}, u32[]{:S(2)}) %collective-permute-start.8) | collective-permute-done | bytes 131104 | tf_op jit(solution)/shard_map/ppermute | solution.py:237
  76.3 25.6 %chain.10 = (f32[512,512]{1,0:T(8,128)}, f32[512,128]{1,0:T(8,128)}) custom-call(f32[512,512]{1,0:T(8,128)} %pad_maximum_fusion.13.s_ref), custom_call_target="tpu_custom_call" | custom-call | flops 2500000000 | bytes 1048576 | tf_op jit(solution)/shard_map/chain/pallas_call | solution.py:100
  108.3 8.9 collective-permute-done.15
  130.6 16.1 %collective-permute-done.12 = f32[8,128,256]{2,1,0:T(8,128)S(1)} collective-permute-done((f32[8,128,256]{2,1,0:T(8,128)S(1)}, f32[8,128,256]{2,1,0:T(8,128)S(1)}, u32[]{:S(2)}, u32[]{:S(2)}) %collective-permute-start.12) | collective-permute-done | bytes 1048608 | tf_op jit(solution)/shard_map/ppermute | solution.py:237
  146.7 19.9 %collective-permute-done.13 = f32[8,128,256]{2,1,0:T(8,128)S(1)} collective-permute-done((f32[8,128,256]{2,1,0:T(8,128)S(1)}, f32[8,128,256]{2,1,0:T(8,128)S(1)}, u32[]{:S(2)}, u32[]{:S(2)}) %collective-permute-start.13) | collective-permute-done | bytes 1048608 | tf_op jit(solution)/shard_map/ppermute | solution.py:237
  175.2 20.9 %solve.9 = (f32[1152,512]{1,0:T(8,128)}, f32[512,512]{1,0:T(8,128)}, f32[1024,512]{1,0:T(8,128)}) custom-call(s32[1]{0:T(128)} %bitcast.1.refs_0_, f32[512,512]{1,0:T(8,128)} %get-tuple-element.77.refs_1_, f32[512,128]{1,0:T(8,128)} %get-tuple-element.78.refs_2_, f32[128,512]{1,0:T(8,128)} %copy-done.23, f32[128,512]{1,0:T(8,128)} %copy-done.45, ...), custom_call_target="tpu_custom_call" | custom-call | flops 1610612736 | bytes 1048576 | tf_op jit(solution)/shard_map/solve/pallas_call | solution.py:152
  203.9 25.4 %chain.11 = (f32[512,512]{1,0:T(8,128)}, f32[512,128]{1,0:T(8,128)}) custom-call(f32[512,512]{1,0:T(8,128)} %get-tuple-element.80.s_ref), custom_call_target="tpu_custom_call" | custom-call | flops 2500000000 | bytes 1048576 | tf_op jit(solution)/shard_map/chain/pallas_call | solution.py:100
  243.0 4.1 update.15.refs_7_
  250.8 4.8 collective-permute-done.23.refs_9_
  260.0 7.6 update.16.refs_12_
  270.4 19.4 %solve.10 = (f32[1024,512]{1,0:T(8,128)}, f32[512,512]{1,0:T(8,128)}, f32[896,512]{1,0:T(8,128)}) custom-call(s32[1]{0:T(128)} %bitcast.1.refs_0_, f32[512,512]{1,0:T(8,128)} %get-tuple-element.82.refs_1_, f32[512,128]{1,0:T(8,128)} %get-tuple-element.83.refs_2_, f32[128,512]{1,0:T(8,128)} %copy-done.41, f32[128,512]{1,0:T(8,128)} %collective-permute-done.16.refs_4_, ...), custom_call_target="tpu_custom_call" | custom-call | flops 1476395008 | bytes 1048576 | tf_op jit(solution)/shard_map/solve/pallas_call | solution.py:152
  302.1 4.4 fusion.3
  313.4 29.4 %collective-permute-done.28.refs_5_ = f32[128,512]{1,0:T(8,128)} collective-permute-done((f32[128,512]{1,0:T(8,128)}, f32[128,512]{1,0:T(8,128)}, u32[]{:S(2)}, u32[]{:S(2)}) %collective-permute-start.28) | collective-permute-done | bytes 262176 | tf_op jit(solution)/shard_map/ppermute | solution.py:227
  349.8 25.4 %chain.12 = (f32[512,512]{1,0:T(8,128)}, f32[512,128]{1,0:T(8,128)}) custom-call(f32[512,512]{1,0:T(8,128)} %get-tuple-element.89.s_ref), custom_call_target="tpu_custom_call" | custom-call | flops 2500000000 | bytes 1048576 | tf_op jit(solution)/shard_map/chain/pallas_call | solution.py:100
  390.2 5.4 update.17.refs_7_
  399.8 4.1 collective-permute-done.37.refs_9_
  405.0 9.6 update.18.refs_12_
  415.5 17.9 %solve.11 = (f32[896,512]{1,0:T(8,128)}, f32[512,512]{1,0:T(8,128)}, f32[768,512]{1,0:T(8,128)}) custom-call(s32[1]{0:T(128)} %bitcast.1.refs_0_, f32[512,512]{1,0:T(8,128)} %get-tuple-element.91.refs_1_, f32[512,128]{1,0:T(8,128)} %get-tuple-element.92.refs_2_, f32[128,512]{1,0:T(8,128)} %slice.452.refs_3_, f32[128,512]{1,0:T(8,128)} %copy-done.49, ...), custom_call_target="tpu_custom_call" | custom-call | flops 1342177280 | bytes 1048576 | tf_op jit(solution)/shard_map/solve/pallas_call | solution.py:152
  436.2 25.4 %chain.13 = (f32[512,512]{1,0:T(8,128)}, f32[512,128]{1,0:T(8,128)}) custom-call(f32[512,512]{1,0:T(8,128)} %get-tuple-element.98.s_ref), custom_call_target="tpu_custom_call" | custom-call | flops 2500000000 | bytes 1048576 | tf_op jit(solution)/shard_map/chain/pallas_call | solution.py:100
  475.1 5.1 fusion.4
  482.2 6.5 update.19.refs_7_
  493.7 12.5 %collective-permute-done.42.refs_5_ = f32[128,512]{1,0:T(8,128)} collective-permute-done((f32[128,512]{1,0:T(8,128)}, f32[128,512]{1,0:T(8,128)}, u32[]{:S(2)}, u32[]{:S(2)}) %collective-permute-start.42) | collective-permute-done | bytes 262176 | tf_op jit(solution)/shard_map/ppermute | solution.py:227
  506.7 4.4 collective-permute-done.51.refs_9_
  513.7 11.0 %update.20.refs_12_ = f32[640,512]{1,0:T(8,128)} custom-call(s32[1]{0:T(128)} %bitcast.1.refs_0_, f32[640,512]{1,0:T(8,128)} %slice.469.refs_1_, f32[1152,512]{1,0:T(8,128)} %get-tuple-element.79.refs_2_.refs_3_.refs_4_.refs_5_.refs_6_.refs_7_.refs_8_.refs_9_.refs_10_, ...), custom_call_target="tpu_custom_call" | custom-call | flops 2013265920 | bytes 1048576 | tf_op jit(solution)/shard_map/update/pallas_call | solution.py:195
  525.8 16.0 %solve.12 = (f32[768,512]{1,0:T(8,128)}, f32[512,512]{1,0:T(8,128)}, f32[640,512]{1,0:T(8,128)}) custom-call(s32[1]{0:T(128)} %bitcast.1.refs_0_, f32[512,512]{1,0:T(8,128)} %get-tuple-element.100.refs_1_, f32[512,128]{1,0:T(8,128)} %get-tuple-element.101.refs_2_, f32[128,512]{1,0:T(8,128)} %slice.465.refs_3_, f32[128,512]{1,0:T(8,128)} %collective-permute-done.41.refs_4_, ...), custom_call_target="tpu_custom_call" | custom-call | flops 1207959552 | bytes 1048576 | tf_op jit(solution)/shard_map/solve/pallas_call | solution.py:152
  565.4 25.7 %chain.14 = (f32[512,512]{1,0:T(8,128)}, f32[512,128]{1,0:T(8,128)}) custom-call(f32[512,512]{1,0:T(8,128)} %get-tuple-element.107.s_ref), custom_call_target="tpu_custom_call" | custom-call | flops 2500000000 | bytes 1048576 | tf_op jit(solution)/shard_map/chain/pallas_call | solution.py:100
  594.8 7.7 update.21.refs_7_
  612.8 11.6 %update.22.refs_12_ = f32[512,512]{1,0:T(8,128)} custom-call(s32[1]{0:T(128)} %bitcast.1.refs_0_, f32[512,512]{1,0:T(8,128)} %slice.482.refs_1_, f32[1152,512]{1,0:T(8,128)} %get-tuple-element.79.refs_2_.refs_3_.refs_4_.refs_5_.refs_6_.refs_7_.refs_8_.refs_9_.refs_10_, ...), custom_call_target="tpu_custom_call" | custom-call | flops 2147483648 | bytes 1048576 | tf_op jit(solution)/shard_map/update/pallas_call | solution.py:195
  626.5 14.5 %solve.13 = (f32[640,512]{1,0:T(8,128)}, f32[512,512]{1,0:T(8,128)}, f32[512,512]{1,0:T(8,128)}) custom-call(s32[1]{0:T(128)} %bitcast.1.refs_0_, f32[512,512]{1,0:T(8,128)} %get-tuple-element.109.refs_1_, f32[512,128]{1,0:T(8,128)} %get-tuple-element.110.refs_2_, f32[128,512]{1,0:T(8,128)} %copy-done.38, f32[128,512]{1,0:T(8,128)} %copy-done.53, ...), custom_call_target="tpu_custom_call" | custom-call | flops 1073741824 | bytes 1048576 | tf_op jit(solution)/shard_map/solve/pallas_call | solution.py:152
  664.7 25.6 %chain.15 = (f32[512,512]{1,0:T(8,128)}, f32[512,128]{1,0:T(8,128)}) custom-call(f32[512,512]{1,0:T(8,128)} %get-tuple-element.116.s_ref), custom_call_target="tpu_custom_call" | custom-call | flops 2500000000 | bytes 1048576 | tf_op jit(solution)/shard_map/chain/pallas_call | solution.py:100
  697.0 8.9 update.23.refs_7_
  707.9 11.3 %update.24.refs_12_ = f32[384,512]{1,0:T(8,128)} custom-call(s32[1]{0:T(128)} %bitcast.1.refs_0_, f32[384,512]{1,0:T(8,128)} %slice.495.refs_1_, f32[1152,512]{1,0:T(8,128)} %get-tuple-element.79.refs_2_.refs_3_.refs_4_.refs_5_.refs_6_.refs_7_.refs_8_.refs_9_.refs_10_, ...), custom_call_target="tpu_custom_call" | custom-call | flops 2013265920 | bytes 1048576 | tf_op jit(solution)/shard_map/update/pallas_call | solution.py:195
  727.2 13.0 %solve.14 = (f32[512,512]{1,0:T(8,128)}, f32[512,512]{1,0:T(8,128)}, f32[384,512]{1,0:T(8,128)}) custom-call(s32[1]{0:T(128)} %bitcast.1.refs_0_, f32[512,512]{1,0:T(8,128)} %get-tuple-element.118.refs_1_, f32[512,128]{1,0:T(8,128)} %get-tuple-element.119.refs_2_, f32[128,512]{1,0:T(8,128)} %slice.491.refs_3_, f32[128,512]{1,0:T(8,128)} %copy-done.73, ...), custom_call_target="tpu_custom_call" | custom-call | flops 939524096 | bytes 1048576 | tf_op jit(solution)/shard_map/solve/pallas_call | solution.py:152
  759.3 25.6 %chain.16 = (f32[512,512]{1,0:T(8,128)}, f32[512,128]{1,0:T(8,128)}) custom-call(f32[512,512]{1,0:T(8,128)} %get-tuple-element.125.s_ref), custom_call_target="tpu_custom_call" | custom-call | flops 2500000000 | bytes 1048576 | tf_op jit(solution)/shard_map/chain/pallas_call | solution.py:100
  792.0 10.1 update.25.refs_7_
  804.1 9.8 update.26.refs_12_
  818.4 11.4 %solve.15 = (f32[384,512]{1,0:T(8,128)}, f32[512,512]{1,0:T(8,128)}, f32[256,512]{1,0:T(8,128)}) custom-call(s32[1]{0:T(128)} %bitcast.1.refs_0_, f32[512,512]{1,0:T(8,128)} %get-tuple-element.127.refs_1_, f32[512,128]{1,0:T(8,128)} %get-tuple-element.128.refs_2_, f32[128,512]{1,0:T(8,128)} %slice.504.refs_3_, f32[128,512]{1,0:T(8,128)} %copy-done.48, ...), custom_call_target="tpu_custom_call" | custom-call | flops 805306368 | bytes 1048576 | tf_op jit(solution)/shard_map/solve/pallas_call | solution.py:152
  840.2 25.6 %chain.17 = (f32[512,512]{1,0:T(8,128)}, f32[512,128]{1,0:T(8,128)}) custom-call(f32[512,512]{1,0:T(8,128)} %get-tuple-element.134.s_ref), custom_call_target="tpu_custom_call" | custom-call | flops 2500000000 | bytes 1048576 | tf_op jit(solution)/shard_map/chain/pallas_call | solution.py:100
  874.0 11.4 %update.27.refs_7_ = f32[128,512]{1,0:T(8,128)} custom-call(s32[1]{0:T(128)} %bitcast.1.refs_0_, f32[128,512]{1,0:T(8,128)} %get-tuple-element.272.refs_1_, f32[1152,512]{1,0:T(8,128)} %get-tuple-element.79.refs_2_.refs_3_.refs_4_.refs_5_.refs_6_.refs_7_.refs_8_.refs_9_.refs_10_, ...), custom_call_target="tpu_custom_call" | custom-call | flops 939524096 | bytes 1048576 | tf_op jit(solution)/shard_map/update/pallas_call | solution.py:195
  890.6 4.0 collective-permute-done.107.refs_9_
  895.8 11.7 %update.28.refs_12_ = f32[128,512]{1,0:T(8,128)} custom-call(s32[1]{0:T(128)} %bitcast.1.refs_0_, f32[128,512]{1,0:T(8,128)} %get-tuple-element.141.refs_1_, f32[1152,512]{1,0:T(8,128)} %get-tuple-element.79.refs_2_.refs_3_.refs_4_.refs_5_.refs_6_.refs_7_.refs_8_.refs_9_.refs_10_, ...), custom_call_target="tpu_custom_call" | custom-call | flops 939524096 | bytes 1048576 | tf_op jit(solution)/shard_map/update/pallas_call | solution.py:195
  910.0 10.4 %solve.16 = (f32[256,512]{1,0:T(8,128)}, f32[512,512]{1,0:T(8,128)}, f32[128,512]{1,0:T(8,128)}) custom-call(s32[1]{0:T(128)} %bitcast.1.refs_0_, f32[512,512]{1,0:T(8,128)} %get-tuple-element.136.refs_1_, f32[512,128]{1,0:T(8,128)} %get-tuple-element.137.refs_2_, f32[128,512]{1,0:T(8,128)} %slice.517.refs_3_, f32[128,512]{1,0:T(8,128)} %copy-done.51, ...), custom_call_target="tpu_custom_call" | custom-call | flops 671088640 | bytes 1048576 | tf_op jit(solution)/shard_map/solve/pallas_call | solution.py:152
  925.4 5.3 collective-permute-done.118.refs_40_
  931.6 25.5 %chain.18 = (f32[512,512]{1,0:T(8,128)}, f32[512,128]{1,0:T(8,128)}) custom-call(f32[512,512]{1,0:T(8,128)} %get-tuple-element.143.s_ref), custom_call_target="tpu_custom_call" | custom-call | flops 2500000000 | bytes 1048576 | tf_op jit(solution)/shard_map/chain/pallas_call | solution.py:100
  958.8 12.5 %update.29.refs_7_ = f32[128,512]{1,0:T(8,128)} custom-call(s32[1]{0:T(128)} %bitcast.1.refs_0_, f32[128,512]{1,0:T(8,128)} %maximum_bitcast_fusion.3.refs_1_, f32[1152,512]{1,0:T(8,128)} %get-tuple-element.79.refs_2_.refs_3_.refs_4_.refs_5_.refs_6_.refs_7_.refs_8_.refs_9_.refs_10_, ...), custom_call_target="tpu_custom_call" | custom-call | flops 1073741824 | bytes 1048576 | tf_op jit(solution)/shard_map/update/pallas_call | solution.py:195
  975.5 4.0 collective-permute-done.121.refs_9_
  981.8 9.0 solve.17
  995.6 25.4 %chain.19 = (f32[512,512]{1,0:T(8,128)}, f32[512,128]{1,0:T(8,128)}) custom-call(f32[512,512]{1,0:T(8,128)} %get-tuple-element.150.s_ref), custom_call_target="tpu_custom_call" | custom-call | flops 2500000000 | bytes 1048576 | tf_op jit(solution)/shard_map/chain/pallas_call | solution.py:100
  (573 shorter events, 351.3 us)
Async XLA Ops:
  1.7 57.4 %collective-permute-start.96 = (f32[2,128,256]{2,1,0:T(8,128)S(1)}, f32[2,128,256]{2,1,0:T(8,128)S(1)}, u32[]{:S(2)}, u32[]{:S(2)}) collective-permute-start(f32[2,128,256]{2,1,0:T(8,128)S(1)} %slice_select_fusion.16), channel_id=1, source_target_pairs={{0,4},{4,0},{1,5},{5,1},{2,6},{6,2},{3,7},{7,3}} | collective-permute-start | bytes 786440 | tf_op jit(solution)/shard_map/ppermute | solution.py:237
  10.4 51.8 %collective-permute-start.82 = (f32[3,128,256]{2,1,0:T(8,128)}, f32[3,128,256]{2,1,0:T(8,128)}, u32[]{:S(2)}, u32[]{:S(2)}) collective-permute-start(f32[3,128,256]{2,1,0:T(8,128)} %slice_select_fusion.14), channel_id=1, source_target_pairs={{0,4},{4,0},{1,5},{5,1},{2,6},{6,2},{3,7},{7,3}} | collective-permute-start | bytes 1179656 | tf_op jit(solution)/shard_map/ppermute | solution.py:237
  22.6 46.5 %collective-permute-start.68 = (f32[4,128,256]{2,1,0:T(8,128)S(1)}, f32[4,128,256]{2,1,0:T(8,128)S(1)}, u32[]{:S(2)}, u32[]{:S(2)}) collective-permute-start(f32[4,128,256]{2,1,0:T(8,128)S(1)} %slice_select_fusion.12), channel_id=1, source_target_pairs={{0,4},{4,0},{1,5},{5,1},{2,6},{6,2},{3,7},{7,3}} | collective-permute-start | bytes 1572872 | tf_op jit(solution)/shard_map/ppermute | solution.py:237
  22.6 80.9 %collective-permute-start.54 = (f32[5,128,256]{2,1,0:T(8,128)}, f32[5,128,256]{2,1,0:T(8,128)}, u32[]{:S(2)}, u32[]{:S(2)}) collective-permute-start(f32[5,128,256]{2,1,0:T(8,128)} %slice_select_fusion.10), channel_id=1, source_target_pairs={{0,4},{4,0},{1,5},{5,1},{2,6},{6,2},{3,7},{7,3}} | collective-permute-start | bytes 1966088 | tf_op jit(solution)/shard_map/ppermute | solution.py:237
  56.3 50.1 %collective-permute-start.40 = (f32[6,128,256]{2,1,0:T(8,128)}, f32[6,128,256]{2,1,0:T(8,128)}, u32[]{:S(2)}, u32[]{:S(2)}) collective-permute-start(f32[6,128,256]{2,1,0:T(8,128)} %slice_select_fusion.8), channel_id=1, source_target_pairs={{0,4},{4,0},{1,5},{5,1},{2,6},{6,2},{3,7},{7,3}} | collective-permute-start | bytes 2359304 | tf_op jit(solution)/shard_map/ppermute | solution.py:237
  59.1 65.1 %collective-permute-start.26 = (f32[7,128,256]{2,1,0:T(8,128)}, f32[7,128,256]{2,1,0:T(8,128)S(1)}, u32[]{:S(2)}, u32[]{:S(2)}) collective-permute-start(f32[7,128,256]{2,1,0:T(8,128)} %slice_select_fusion.6), channel_id=1, source_target_pairs={{0,4},{4,0},{1,5},{5,1},{2,6},{6,2},{3,7},{7,3}} | collective-permute-start | bytes 2752520 | tf_op jit(solution)/shard_map/ppermute | solution.py:237
  72.1 45.1 %collective-permute-start.15 = (f32[8,128,256]{2,1,0:T(8,128)S(1)}, f32[8,128,256]{2,1,0:T(8,128)S(1)}, u32[]{:S(2)}, u32[]{:S(2)}) collective-permute-start(f32[8,128,256]{2,1,0:T(8,128)S(1)} %slice_select_fusion), channel_id=1, source_target_pairs={{0,4},{4,0},{1,5},{5,1},{2,6},{6,2},{3,7},{7,3}} | collective-permute-start | bytes 3145736 | tf_op jit(solution)/shard_map/ppermute | solution.py:237
  73.6 56.1 %collective-permute-start.6 = (f32[128,512]{1,0:T(8,128)S(1)}, f32[128,512]{1,0:T(8,128)}, u32[]{:S(2)}, u32[]{:S(2)}) collective-permute-start(f32[128,512]{1,0:T(8,128)S(1)} %maximum_bitcast_fusion.1.refs_3_), channel_id=1, source_target_pairs={{0,2},{1,3},{2,0},{3,1},{4,6},{5,7},{6,4},{7,5}} | collective-permute-start | bytes 786440 | tf_op jit(solution)/shard_map/ppermute | solution.py:227
  103.6 69.5 %collective-permute-start.5 = (f32[128,512]{1,0:T(8,128)S(1)}, f32[128,512]{1,0:T(8,128)S(1)}, u32[]{:S(2)}, u32[]{:S(2)}) collective-permute-start(f32[128,512]{1,0:T(8,128)S(1)} %maximum_bitcast_fusion.1.refs_3_), channel_id=1, source_target_pairs={{0,1},{1,0},{2,3},{3,2},{4,5},{5,4},{6,7},{7,6}} | collective-permute-start | bytes 786440 | tf_op jit(solution)/shard_map/ppermute | solution.py:227
  122.1 44.5 %collective-permute-start.13 = (f32[8,128,256]{2,1,0:T(8,128)S(1)}, f32[8,128,256]{2,1,0:T(8,128)S(1)}, u32[]{:S(2)}, u32[]{:S(2)}) collective-permute-start(f32[8,128,256]{2,1,0:T(8,128)S(1)} %get-tuple-element.189), channel_id=1, source_target_pairs={{0,4},{4,0},{1,5},{5,1},{2,6},{6,2},{3,7},{7,3}} | collective-permute-start | bytes 3145736 | tf_op jit(solution)/shard_map/ppermute | solution.py:237
  129.6 44.2 %collective-permute-start.9 = (f32[128,512]{1,0:T(8,128)}, f32[128,512]{1,0:T(8,128)S(1)}, u32[]{:S(2)}, u32[]{:S(2)}) collective-permute-start(f32[128,512]{1,0:T(8,128)} %maximum_bitcast_fusion.2.refs_7_), channel_id=1, source_target_pairs={{0,1},{1,0},{2,3},{3,2},{4,5},{5,4},{6,7},{7,6}} | collective-permute-start | bytes 786440 | tf_op jit(solution)/shard_map/ppermute | solution.py:227
  130.6 43.2 %collective-permute-start.7 = (f32[128,512]{1,0:T(8,128)}, f32[128,512]{1,0:T(8,128)S(1)}, u32[]{:S(2)}, u32[]{:S(2)}) collective-permute-start(f32[128,512]{1,0:T(8,128)} %collective-permute-done.6.refs_5_), channel_id=1, source_target_pairs={{0,1},{1,0},{2,3},{3,2},{4,5},{5,4},{6,7},{7,6}} | collective-permute-start | bytes 786440 | tf_op jit(solution)/shard_map/ppermute | solution.py:227
  197.8 38.5 %collective-permute-start.20 = (f32[128,512]{1,0:T(8,128)}, f32[128,512]{1,0:T(8,128)}, u32[]{:S(2)}, u32[]{:S(2)}) collective-permute-start(f32[128,512]{1,0:T(8,128)} %slice.442), channel_id=1, source_target_pairs={{0,2},{1,3},{2,0},{3,1},{4,6},{5,7},{6,4},{7,5}} | collective-permute-start | bytes 786440 | tf_op jit(solution)/shard_map/ppermute | solution.py:227
  203.0 98.8 %collective-permute-start.31 = (f32[896,512]{1,0:T(8,128)}, f32[896,512]{1,0:T(8,128)}, u32[]{:S(2)}, u32[]{:S(2)}) collective-permute-start(f32[896,512]{1,0:T(8,128)} %slice.454), channel_id=1, source_target_pairs={{0,2},{1,3},{2,0},{3,1},{4,6},{5,7},{6,4},{7,5}} | collective-permute-start | bytes 5505032 | tf_op jit(solution)/shard_map/ppermute | solution.py:227
  267.5 120.9 %collective-permute-start.30 = (f32[896,512]{1,0:T(8,128)}, f32[896,512]{1,0:T(8,128)}, u32[]{:S(2)}, u32[]{:S(2)}) collective-permute-start(f32[896,512]{1,0:T(8,128)} %slice.454), channel_id=1, source_target_pairs={{0,1},{1,0},{2,3},{3,2},{4,5},{5,4},{6,7},{7,6}} | collective-permute-start | bytes 5505032 | tf_op jit(solution)/shard_map/ppermute | solution.py:227
  268.1 116.4 %collective-permute-start.14 = (f32[10,128,256]{2,1,0:T(8,128)}, f32[10,128,256]{2,1,0:T(8,128)}, u32[]{:S(2)}, u32[]{:S(2)}) collective-permute-start(f32[10,128,256]{2,1,0:T(8,128)} %select_n.654), channel_id=1, source_target_pairs={{0,4},{4,0},{1,5},{5,1},{2,6},{6,2},{3,7},{7,3}} | collective-permute-start | bytes 3932168 | tf_op jit(solution)/shard_map/ppermute | solution.py:268
  300.4 88.1 %collective-permute-start.45 = (f32[768,512]{1,0:T(8,128)}, f32[768,512]{1,0:T(8,128)S(1)}, u32[]{:S(2)}, u32[]{:S(2)}) collective-permute-start(f32[768,512]{1,0:T(8,128)} %slice.467), channel_id=1, source_target_pairs={{0,2},{1,3},{2,0},{3,1},{4,6},{5,7},{6,4},{7,5}} | collective-permute-start | bytes 4718600 | tf_op jit(solution)/shard_map/ppermute | solution.py:227
  301.9 87.0 %collective-permute-start.32 = (f32[896,512]{1,0:T(8,128)}, f32[896,512]{1,0:T(8,128)S(1)}, u32[]{:S(2)}, u32[]{:S(2)}) collective-permute-start(f32[896,512]{1,0:T(8,128)} %collective-permute-done.31.refs_6_.refs_7_.refs_8_.refs_9_.refs_10_.refs_11_.refs_12_), channel_id=1, source_target_pairs={{0,1},{1,0},{2,3},{3,2},{4,5},{5,4},{6,7},{7,6}} | collective-permute-start | bytes 5505032 | tf_op jit(solution)/shard_map/ppermute | solution.py:227
  308.2 34.6 %collective-permute-start.28 = (f32[128,512]{1,0:T(8,128)}, f32[128,512]{1,0:T(8,128)}, u32[]{:S(2)}, u32[]{:S(2)}) collective-permute-start(f32[128,512]{1,0:T(8,128)} %slice.452.refs_3_), channel_id=1, source_target_pairs={{0,2},{1,3},{2,0},{3,1},{4,6},{5,7},{6,4},{7,5}} | collective-permute-start | bytes 786440 | tf_op jit(solution)/shard_map/ppermute | solution.py:227
  342.8 52.8 %collective-permute-start.25 = (f32[9,128,256]{2,1,0:T(8,128)}, f32[9,128,256]{2,1,0:T(8,128)}, u32[]{:S(2)}, u32[]{:S(2)}) collective-permute-start(f32[9,128,256]{2,1,0:T(8,128)} %select_n.665), channel_id=1, source_target_pairs={{0,4},{4,0},{1,5},{5,1},{2,6},{6,2},{3,7},{7,3}} | collective-permute-start | bytes 3538952 | tf_op jit(solution)/shard_map/ppermute | solution.py:268
  388.4 91.7 %collective-permute-start.44 = (f32[768,512]{1,0:T(8,128)}, f32[768,512]{1,0:T(8,128)}, u32[]{:S(2)}, u32[]{:S(2)}) collective-permute-start(f32[768,512]{1,0:T(8,128)} %slice.467), channel_id=1, source_target_pairs={{0,1},{1,0},{2,3},{3,2},{4,5},{5,4},{6,7},{7,6}} | collective-permute-start | bytes 4718600 | tf_op jit(solution)/shard_map/ppermute | solution.py:227
  388.9 92.4 %collective-permute-start.46 = (f32[768,512]{1,0:T(8,128)S(1)}, f32[768,512]{1,0:T(8,128)}, u32[]{:S(2)}, u32[]{:S(2)}) collective-permute-start(f32[768,512]{1,0:T(8,128)S(1)} %collective-permute-done.45.refs_11_.refs_12_.refs_13_.refs_14_.refs_15_.refs_16_), channel_id=1, source_target_pairs={{0,1},{1,0},{2,3},{3,2},{4,5},{5,4},{6,7},{7,6}} | collective-permute-start | bytes 4718600 | tf_op jit(solution)/shard_map/ppermute | solution.py:227
  435.1 40.0 %collective-permute-start.48 = (f32[128,512]{1,0:T(8,128)}, f32[128,512]{1,0:T(8,128)}, u32[]{:S(2)}, u32[]{:S(2)}) collective-permute-start(f32[128,512]{1,0:T(8,128)} %slice.468), channel_id=1, source_target_pairs={{0,2},{1,3},{2,0},{3,1},{4,6},{5,7},{6,4},{7,5}} | collective-permute-start | bytes 786440 | tf_op jit(solution)/shard_map/ppermute | solution.py:227
  469.0 81.6 %collective-permute-start.59 = (f32[640,512]{1,0:T(8,128)}, f32[640,512]{1,0:T(8,128)}, u32[]{:S(2)}, u32[]{:S(2)}) collective-permute-start(f32[640,512]{1,0:T(8,128)} %slice.480), channel_id=1, source_target_pairs={{0,2},{1,3},{2,0},{3,1},{4,6},{5,7},{6,4},{7,5}} | collective-permute-start | bytes 3932168 | tf_op jit(solution)/shard_map/ppermute | solution.py:227
  512.1 47.0 %collective-permute-start.39 = (f32[8,128,256]{2,1,0:T(8,128)}, f32[8,128,256]{2,1,0:T(8,128)}, u32[]{:S(2)}, u32[]{:S(2)}) collective-permute-start(f32[8,128,256]{2,1,0:T(8,128)} %select_n.676), channel_id=1, source_target_pairs={{0,4},{4,0},{1,5},{5,1},{2,6},{6,2},{3,7},{7,3}} | collective-permute-start | bytes 3145736 | tf_op jit(solution)/shard_map/ppermute | solution.py:268
  524.8 39.5 %collective-permute-start.58 = (f32[640,512]{1,0:T(8,128)}, f32[640,512]{1,0:T(8,128)S(1)}, u32[]{:S(2)}, u32[]{:S(2)}) collective-permute-start(f32[640,512]{1,0:T(8,128)} %slice.480), channel_id=1, source_target_pairs={{0,1},{1,0},{2,3},{3,2},{4,5},{5,4},{6,7},{7,6}} | collective-permute-start | bytes 3932168 | tf_op jit(solution)/shard_map/ppermute | solution.py:227
  550.5 44.3 %collective-permute-start.60 = (f32[640,512]{1,0:T(8,128)}, f32[640,512]{1,0:T(8,128)}, u32[]{:S(2)}, u32[]{:S(2)}) collective-permute-start(f32[640,512]{1,0:T(8,128)} %collective-permute-done.59.refs_16_.refs_17_.refs_18_.refs_19_.refs_20_), channel_id=1, source_target_pairs={{0,1},{1,0},{2,3},{3,2},{4,5},{5,4},{6,7},{7,6}} | collective-permute-start | bytes 3932168 | tf_op jit(solution)/shard_map/ppermute | solution.py:227
  558.3 48.9 %collective-permute-start.53 = (f32[7,128,256]{2,1,0:T(8,128)}, f32[7,128,256]{2,1,0:T(8,128)}, u32[]{:S(2)}, u32[]{:S(2)}) collective-permute-start(f32[7,128,256]{2,1,0:T(8,128)} %select_n.687), channel_id=1, source_target_pairs={{0,4},{4,0},{1,5},{5,1},{2,6},{6,2},{3,7},{7,3}} | collective-permute-start | bytes 2752520 | tf_op jit(solution)/shard_map/ppermute | solution.py:268
  564.3 60.9 %collective-permute-start.73 = (f32[512,512]{1,0:T(8,128)}, f32[512,512]{1,0:T(8,128)}, u32[]{:S(2)}, u32[]{:S(2)}) collective-permute-start(f32[512,512]{1,0:T(8,128)} %slice.493), channel_id=1, source_target_pairs={{0,2},{1,3},{2,0},{3,1},{4,6},{5,7},{6,4},{7,5}} | collective-permute-start | bytes 3145736 | tf_op jit(solution)/shard_map/ppermute | solution.py:227
  624.5 39.3 %collective-permute-start.72 = (f32[512,512]{1,0:T(8,128)}, f32[512,512]{1,0:T(8,128)S(1)}, u32[]{:S(2)}, u32[]{:S(2)}) collective-permute-start(f32[512,512]{1,0:T(8,128)} %slice.493), channel_id=1, source_target_pairs={{0,1},{1,0},{2,3},{3,2},{4,5},{5,4},{6,7},{7,6}} | collective-permute-start | bytes 3145736 | tf_op jit(solution)/shard_map/ppermute | solution.py:227
  625.2 70.6 %collective-permute-start.74 = (f32[512,512]{1,0:T(8,128)}, f32[512,512]{1,0:T(8,128)S(1)}, u32[]{:S(2)}, u32[]{:S(2)}) collective-permute-start(f32[512,512]{1,0:T(8,128)} %collective-permute-done.73.refs_21_.refs_22_.refs_23_.refs_24_), channel_id=1, source_target_pairs={{0,1},{1,0},{2,3},{3,2},{4,5},{5,4},{6,7},{7,6}} | collective-permute-start | bytes 3145736 | tf_op jit(solution)/shard_map/ppermute | solution.py:227
  656.6 64.8 %collective-permute-start.67 = (f32[6,128,256]{2,1,0:T(8,128)}, f32[6,128,256]{2,1,0:T(8,128)}, u32[]{:S(2)}, u32[]{:S(2)}) collective-permute-start(f32[6,128,256]{2,1,0:T(8,128)} %select_n.698), channel_id=1, source_target_pairs={{0,4},{4,0},{1,5},{5,1},{2,6},{6,2},{3,7},{7,3}} | collective-permute-start | bytes 2359304 | tf_op jit(solution)/shard_map/ppermute | solution.py:268
  660.5 35.4 %collective-permute-start.75 = (f32[128,512]{1,0:T(8,128)}, f32[128,512]{1,0:T(8,128)}, u32[]{:S(2)}, u32[]{:S(2)}) collective-permute-start(f32[128,512]{1,0:T(8,128)} %slice.494), channel_id=1, source_target_pairs={{0,1},{1,0},{2,3},{3,2},{4,5},{5,4},{6,7},{7,6}} | collective-permute-start | bytes 786440 | tf_op jit(solution)/shard_map/ppermute | solution.py:227
  660.5 36.5 %collective-permute-start.77 = (f32[128,512]{1,0:T(8,128)}, f32[128,512]{1,0:T(8,128)}, u32[]{:S(2)}, u32[]{:S(2)}) collective-permute-start(f32[128,512]{1,0:T(8,128)} %collective-permute-done.76.refs_25_), channel_id=1, source_target_pairs={{0,1},{1,0},{2,3},{3,2},{4,5},{5,4},{6,7},{7,6}} | collective-permute-start | bytes 786440 | tf_op jit(solution)/shard_map/ppermute | solution.py:227
  663.8 44.0 %collective-permute-start.70 = (f32[128,512]{1,0:T(8,128)}, f32[128,512]{1,0:T(8,128)}, u32[]{:S(2)}, u32[]{:S(2)}) collective-permute-start(f32[128,512]{1,0:T(8,128)} %slice.491.refs_3_), channel_id=1, source_target_pairs={{0,2},{1,3},{2,0},{3,1},{4,6},{5,7},{6,4},{7,5}} | collective-permute-start | bytes 786440 | tf_op jit(solution)/shard_map/ppermute | solution.py:227
  725.3 65.8 %collective-permute-start.88 = (f32[384,512]{1,0:T(8,128)S(1)}, f32[384,512]{1,0:T(8,128)S(1)}, u32[]{:S(2)}, u32[]{:S(2)}) collective-permute-start(f32[384,512]{1,0:T(8,128)S(1)} %collective-permute-done.87.refs_26_.refs_27_.refs_28_), channel_id=1, source_target_pairs={{0,1},{1,0},{2,3},{3,2},{4,5},{5,4},{6,7},{7,6}} | collective-permute-start | bytes 2359304 | tf_op jit(solution)/shard_map/ppermute | solution.py:227
  743.0 47.0 %collective-permute-start.89 = (f32[128,512]{1,0:T(8,128)}, f32[128,512]{1,0:T(8,128)}, u32[]{:S(2)}, u32[]{:S(2)}) collective-permute-start(f32[128,512]{1,0:T(8,128)} %slice.507), channel_id=1, source_target_pairs={{0,1},{1,0},{2,3},{3,2},{4,5},{5,4},{6,7},{7,6}} | collective-permute-start | bytes 786440 | tf_op jit(solution)/shard_map/ppermute | solution.py:227
  754.8 59.1 %collective-permute-start.81 = (f32[5,128,256]{2,1,0:T(8,128)}, f32[5,128,256]{2,1,0:T(8,128)}, u32[]{:S(2)}, u32[]{:S(2)}) collective-permute-start(f32[5,128,256]{2,1,0:T(8,128)} %select_n.709), channel_id=1, source_target_pairs={{0,4},{4,0},{1,5},{5,1},{2,6},{6,2},{3,7},{7,3}} | collective-permute-start | bytes 1966088 | tf_op jit(solution)/shard_map/ppermute | solution.py:268
  755.3 34.7 %collective-permute-start.91 = (f32[128,512]{1,0:T(8,128)}, f32[128,512]{1,0:T(8,128)}, u32[]{:S(2)}, u32[]{:S(2)}) collective-permute-start(f32[128,512]{1,0:T(8,128)} %collective-permute-done.90.refs_30_), channel_id=1, source_target_pairs={{0,1},{1,0},{2,3},{3,2},{4,5},{5,4},{6,7},{7,6}} | collective-permute-start | bytes 786440 | tf_op jit(solution)/shard_map/ppermute | solution.py:227
  758.4 45.7 %collective-permute-start.84 = (f32[128,512]{1,0:T(8,128)}, f32[128,512]{1,0:T(8,128)}, u32[]{:S(2)}, u32[]{:S(2)}) collective-permute-start(f32[128,512]{1,0:T(8,128)} %slice.504.refs_3_), channel_id=1, source_target_pairs={{0,2},{1,3},{2,0},{3,1},{4,6},{5,7},{6,4},{7,5}} | collective-permute-start | bytes 786440 | tf_op jit(solution)/shard_map/ppermute | solution.py:227
  816.9 55.2 %collective-permute-start.100 = (f32[256,512]{1,0:T(8,128)}, f32[256,512]{1,0:T(8,128)S(1)}, u32[]{:S(2)}, u32[]{:S(2)}) collective-permute-start(f32[256,512]{1,0:T(8,128)} %slice.519), channel_id=1, source_target_pairs={{0,1},{1,0},{2,3},{3,2},{4,5},{5,4},{6,7},{7,6}} | collective-permute-start | bytes 1572872 | tf_op jit(solution)/shard_map/ppermute | solution.py:227
  817.3 55.9 %collective-permute-start.102 = (f32[256,512]{1,0:T(8,128)S(1)}, f32[256,512]{1,0:T(8,128)S(1)}, u32[]{:S(2)}, u32[]{:S(2)}) collective-permute-start(f32[256,512]{1,0:T(8,128)S(1)} %collective-permute-done.101.refs_31_.refs_32_), channel_id=1, source_target_pairs={{0,1},{1,0},{2,3},{3,2},{4,5},{5,4},{6,7},{7,6}} | collective-permute-start | bytes 1572872 | tf_op jit(solution)/shard_map/ppermute | solution.py:227
  832.8 40.5 %collective-permute-start.103 = (f32[128,512]{1,0:T(8,128)}, f32[128,512]{1,0:T(8,128)}, u32[]{:S(2)}, u32[]{:S(2)}) collective-permute-start(f32[128,512]{1,0:T(8,128)} %get-tuple-element.256), channel_id=1, source_target_pairs={{0,1},{1,0},{2,3},{3,2},{4,5},{5,4},{6,7},{7,6}} | collective-permute-start | bytes 786440 | tf_op jit(solution)/shard_map/ppermute | solution.py:227
  908.8 48.4 %collective-permute-start.114 = (f32[128,512]{1,0:T(8,128)}, f32[128,512]{1,0:T(8,128)S(1)}, u32[]{:S(2)}, u32[]{:S(2)}) collective-permute-start(f32[128,512]{1,0:T(8,128)} %get-tuple-element.255), channel_id=1, source_target_pairs={{0,1},{1,0},{2,3},{3,2},{4,5},{5,4},{6,7},{7,6}} | collective-permute-start | bytes 786440 | tf_op jit(solution)/shard_map/ppermute | solution.py:227
  909.2 48.9 %collective-permute-start.116 = (f32[128,512]{1,0:T(8,128)S(1)}, f32[128,512]{1,0:T(8,128)S(1)}, u32[]{:S(2)}, u32[]{:S(2)}) collective-permute-start(f32[128,512]{1,0:T(8,128)S(1)} %collective-permute-done.115.refs_36_), channel_id=1, source_target_pairs={{0,1},{1,0},{2,3},{3,2},{4,5},{5,4},{6,7},{7,6}} | collective-permute-start | bytes 786440 | tf_op jit(solution)/shard_map/ppermute | solution.py:227
  923.0 35.1 %collective-permute-start.117 = (f32[128,512]{1,0:T(8,128)}, f32[128,512]{1,0:T(8,128)}, u32[]{:S(2)}, u32[]{:S(2)}) collective-permute-start(f32[128,512]{1,0:T(8,128)} %slice.531), channel_id=1, source_target_pairs={{0,1},{1,0},{2,3},{3,2},{4,5},{5,4},{6,7},{7,6}} | collective-permute-start | bytes 786440 | tf_op jit(solution)/shard_map/ppermute | solution.py:227
  931.1 48.5 %collective-permute-start.109 = (f32[3,128,256]{2,1,0:T(8,128)S(1)}, f32[3,128,256]{2,1,0:T(8,128)S(1)}, u32[]{:S(2)}, u32[]{:S(2)}) collective-permute-start(f32[3,128,256]{2,1,0:T(8,128)S(1)} %select_n.731), channel_id=1, source_target_pairs={{0,4},{4,0},{1,5},{5,1},{2,6},{6,2},{3,7},{7,3}} | collective-permute-start | bytes 1179656 | tf_op jit(solution)/shard_map/ppermute | solution.py:268
  994.1 33.8 %collective-permute-start.123 = (f32[2,128,256]{2,1,0:T(8,128)S(1)}, f32[2,128,256]{2,1,0:T(8,128)S(1)}, u32[]{:S(2)}, u32[]{:S(2)}) collective-permute-start(f32[2,128,256]{2,1,0:T(8,128)S(1)} %select_n.741), channel_id=1, source_target_pairs={{0,4},{4,0},{1,5},{5,1},{2,6},{6,2},{3,7},{7,3}} | collective-permute-start | bytes 786440 | tf_op jit(solution)/shard_map/ppermute | solution.py:268
  (157 other events, 1806.9 us)

commit v2 on v1

v2 whole, which is shorter than its diff:
```python
import functools

import jax
import jax.numpy as jnp
from jax import lax
from jax.experimental import pallas as pl
from jax.experimental.pallas import tpu as pltpu
from jax.sharding import PartitionSpec as P


PRECISE = lax.Precision.HIGHEST
NB = 128
VMEM_SPEC = pl.BlockSpec(memory_space=pltpu.VMEM)
HBM_SPEC = pl.BlockSpec(memory_space=pltpu.HBM)
SMEM_SPEC = pl.BlockSpec(memory_space=pltpu.SMEM)
LIMIT = 60 * 1024 * 1024


def nt(a, b):
    return lax.dot_general(a, b, (((1,), (1,)), ((), ())), precision=PRECISE, preferred_element_type=jnp.float32)


def factor_128(block):
    lane = lax.broadcasted_iota(jnp.int32, (8, 128), 1)
    sub = lax.broadcasted_iota(jnp.int32, (8, 128), 0)
    wide = (8, 128)
    rows = [block[8 * q:8 * q + 8, :] for q in range(16)]
    done, diag_parts = [], []
    for p in range(16):
        cur = rows[p]
        lo = 8 * p
        inside = jnp.logical_and(lane >= lo, lane < lo + 8)
        cols = [jnp.broadcast_to(cur[:, lo + j:lo + j + 1], wide) for j in range(8)]
        has_next = p < 15
        if has_next:
            nxt = rows[p + 1]
            ncols = [jnp.broadcast_to(nxt[:, lo + j:lo + j + 1], wide) for j in range(8)]
            nxt = jnp.where(inside, 0.0, nxt)
        cur = jnp.where(inside, jnp.where(lane - lo == sub, 1.0, 0.0), cur)
        diag_part = jnp.zeros(wide, jnp.float32)
        for j in range(8):
            pivot = jnp.broadcast_to(cols[j][j:j + 1, :], wide)
            inv_root = lax.rsqrt(pivot)
            lcol = cols[j] * inv_root
            for m in range(j + 1, 8):
                cols[m] = cols[m] - lcol * jnp.broadcast_to(lcol[m:m + 1, :], wide)
            wrow = jnp.broadcast_to(cur[j:j + 1, :], wide) * inv_root
            cur = jnp.where(sub == j, wrow, cur - jnp.where(sub > j, lcol, 0.0) * wrow)
            if has_next:
                ncol = ncols[j] * inv_root
                nxt = nxt - ncol * wrow
                for m in range(j + 1, 8):
                    ncols[m] = ncols[m] - ncol * jnp.broadcast_to(lcol[m:m + 1, :], wide)
            diag_part = jnp.where(jnp.logical_and(lane == lo + j, sub >= j), lcol, diag_part)
        done.append(cur)
        diag_parts.append(diag_part)
        if has_next:
            rows[p + 1] = nxt
        if p < 14:
            flipped = cur.T
            for q in range(p + 2, 16):
                acc = jnp.where(inside, 0.0, rows[q])
                for j in range(8):
                    acc = acc - jnp.broadcast_to(flipped[8 * q:8 * q + 8, j:j + 1], wide) * jnp.broadcast_to(cur[j:j + 1, :], wide)
                rows[q] = acc
    packed = jnp.concatenate(done, axis=0)
    diag8 = jnp.concatenate(diag_parts, axis=0)
    full_lane = lax.broadcasted_iota(jnp.int32, (128, 128), 1) // 8
    full_sub = lax.broadcasted_iota(jnp.int32, (128, 128), 0) // 8
    inverse = jnp.where(full_lane <= full_sub, packed, 0.0)
    upper = jnp.where(full_lane > full_sub, packed, 0.0)
    return upper.T + diag8, inverse


def chain_kernel(*refs):
    l_ref, inv_ref, work = refs[-3:]
    n = work.shape[0] // 128
    if len(refs) == 4:
        work[...] = refs[0][...]
    else:
        me, sub = refs[0][0], refs[1][...]
        for k in range(n):
            work[pl.ds(pl.multiple_of(lax.bitwise_xor(me, k) * NB, NB), NB), :] = refs[2 + k][...]
        work[...] = work[...] - nt(sub, sub)
    rowb = lax.broadcasted_iota(jnp.int32, (n * 128, 128), 0) // 128

    def step(k, _):
        lo = pl.multiple_of(k * 128, 128)
        fac, inv = factor_128(work[pl.ds(lo, 128), pl.ds(lo, 128)])
        inv_ref[pl.ds(lo, 128), :] = inv
        col = nt(work[:, pl.ds(lo, 128)], inv)
        col = jnp.where(rowb > k, col, 0.0)
        l_ref[:, pl.ds(lo, 128)] = col
        l_ref[pl.ds(lo, 128), pl.ds(lo, 128)] = fac
        work[...] = work[...] - nt(col, col)
        return 0

    lax.fori_loop(0, n, step, 0)


def shape_of(*dims):
    return jax.ShapeDtypeStruct(dims, jnp.float32)


def cost(flops):
    return pl.CostEstimate(flops=int(flops), bytes_accessed=1 << 20, transcendentals=0)


def chain(*args):
    n = args[-1].shape[1]
    return pl.pallas_call(
        chain_kernel,
        out_shape=(shape_of(n, n), shape_of(n, NB)),
        in_specs=[VMEM_SPEC] if len(args) == 1 else [SMEM_SPEC] + [VMEM_SPEC] * (len(args) - 1),
        out_specs=(VMEM_SPEC,) * 2,
        scratch_shapes=[pltpu.VMEM((n, n), jnp.float32)],
        cost_estimate=cost(2.5e9),
        name="chain",
    )(*args)


def split_store(dst_kept, dst_sent, rows, col, value_of, per):
    for q in range(per):
        kept = pl.multiple_of((2 * q + col) * NB, NB)
        sent = pl.multiple_of((2 * q + 1 - col) * NB, NB)
        dst_kept[rows, q * NB:(q + 1) * NB] = value_of(kept)
        dst_sent[rows, q * NB:(q + 1) * NB] = value_of(sent)


def solve_kernel(rows_n, ahead, far, sub_lo, *refs):
    me_ref, lss_ref, inv_ref = refs[:3]
    sub_refs = refs[3:3 + rows_n]
    rest = list(refs[3 + rows_n:])
    panel = rest.pop()
    if ahead:
        own_ref, w_ref = rest.pop(0), rest.pop(0)
    lown_ref, sub_ref, kept_ref, sent_ref = rest[:4]
    me, col = me_ref[0], me_ref[1]
    wide = rows_n * NB
    per = rows_n // 2
    for k in range(rows_n):
        lo = pl.multiple_of(lax.bitwise_xor(me, k) * NB, NB)
        panel[pl.ds(lo, NB), :] = sub_refs[k][sub_lo:sub_lo + NB, :]
    if ahead:
        panel[wide:, :] = own_ref[NB:, :]
    for k in range(rows_n):
        cols = slice(k * NB, (k + 1) * NB)
        solved = nt(panel[:, cols], inv_ref[cols, :])
        panel[:, cols] = solved
        if k + 1 < rows_n:
            panel[:, (k + 1) * NB:] = panel[:, (k + 1) * NB:] - nt(solved, lss_ref[(k + 1) * NB:, cols])
    sub = panel[:wide, :]
    sub_ref[...] = sub
    mine = pl.ds(pl.multiple_of(me * NB, NB), NB)
    lown_ref[:NB, :] = panel[mine, :]
    split_store(kept_ref, sent_ref, slice(0, NB), col, lambda lo: lss_ref[mine, pl.ds(lo, NB)], per)
    split_store(kept_ref, sent_ref, slice(NB, 2 * NB), col, lambda lo: panel[mine, pl.ds(lo, NB)], per)
    if ahead:
        wout_ref, near_ref = rest[4:6]
        lown_ref[NB:, :] = panel[wide:, :]
        split_store(kept_ref, sent_ref, slice(2 * NB, None), col, lambda lo: panel[wide:, pl.ds(lo, NB)], per)
        wout_ref[...] = w_ref[...] - nt(panel[wide:, :], sub)
        near_ref[:NB, :] = panel[wide:wide + NB, :]
        near_ref[NB:, :] = wout_ref[:NB, :]
        if far:
            rest[6][...] = panel[wide + NB:, :]


def solve(me, lss, inv, own, sub_rel, sub_lo, w_rest):
    rows_n = len(sub_rel)
    wide = rows_n * NB
    rest = w_rest.shape[0] if w_rest is not None else 0
    ahead, far = rest > 0, rest > NB
    args = [me, lss, inv, *sub_rel]
    outs = [shape_of(NB + rest, wide), shape_of(wide, wide)] + [shape_of(2 * NB + rest, wide // 2)] * 2
    if ahead:
        args += [own, w_rest]
        outs += [shape_of(rest, wide), shape_of(2 * NB, wide)]
        if far:
            outs.append(shape_of(rest - NB, wide))
    return pl.pallas_call(
        functools.partial(solve_kernel, rows_n, ahead, far, sub_lo),
        out_shape=tuple(outs),
        in_specs=[SMEM_SPEC] + [VMEM_SPEC] * (len(args) - 1),
        out_specs=(VMEM_SPEC,) * len(outs),
        scratch_shapes=[pltpu.VMEM((wide + rest, wide), jnp.float32)],
        compiler_params=pltpu.CompilerParams(vmem_limit_bytes=LIMIT),
        cost_estimate=cost(2 * (wide + rest) * wide * wide * 2),
        name="solve",
    )(*args)


def update_kernel(rows_n, target, first_row, terms, high, *refs):
    me_ref, one_ref, two_ref, got_ref = refs[:4]
    count = len(terms)
    left_refs = refs[4:4 + count]
    right_refs = refs[4 + count:4 + count + count * rows_n]
    outs = refs[4 + count + count * rows_n:-6]
    acc, left, right, raw, sem, raw_sem = refs[-6:]
    me, col = me_ref[0], me_ref[1]
    wide = rows_n * NB
    half = wide // 2
    height = high * NB
    pending = []
    theirs = pltpu.make_async_copy(got_ref.at[pl.ds(first_row - target, high)], raw.at[1], raw_sem.at[1])
    theirs.start()
    for i, (left_lo, right_los) in enumerate(terms):
        copies = [pltpu.make_async_copy(left_refs[i].at[pl.ds(left_lo, height), :], left.at[i], sem.at[i, rows_n])]
        for k in range(rows_n):
            lo = pl.multiple_of(lax.bitwise_xor(me, k) * NB, NB)
            copies.append(pltpu.make_async_copy(
                right_refs[i * rows_n + k].at[pl.ds(right_los[k], NB), :], right.at[i, pl.ds(lo, NB), :], sem.at[i, k]))
        for copy in copies:
            copy.start()
        pending.append(copies)
    for which, ref in ((0, one_ref), (1, two_ref)):
        @pl.when(col == which)
        def _(ref=ref):
            mine = pltpu.make_async_copy(
                ref.at[pl.ds(first_row, high), :, pl.ds(target * half, half)], raw.at[0], raw_sem.at[0])
            mine.start()
            mine.wait()
    theirs.wait()
    for q in range(rows_n // 2):
        cols = slice(q * NB, (q + 1) * NB)
        acc[:, pl.ds(pl.multiple_of((2 * q + col) * NB, NB), NB)] = raw[0, :, :, cols].reshape(height, NB)
        acc[:, pl.ds(pl.multiple_of((2 * q + 1 - col) * NB, NB), NB)] = raw[1, :, :, cols].reshape(height, NB)
    for i in range(count):
        for copy in pending[i]:
            copy.wait()
        acc[...] = acc[...] - nt(left[i], right[i])
    outs[0][...] = acc[:NB, :]
    if high > 1:
        outs[1][...] = acc[NB:, :]


def update(me, mats, got, target, first_row, high, lefts, rights, terms):
    rows_n = len(rights[0])
    wide = rows_n * NB
    height = high * NB
    count = len(terms)
    args = [me, *mats, got, *lefts, *[piece for group in rights for piece in group]]
    return pl.pallas_call(
        functools.partial(update_kernel, rows_n, target, first_row, terms, high),
        out_shape=(shape_of(NB, wide),) + ((shape_of(height - NB, wide),) if high > 1 else ()),
        in_specs=[SMEM_SPEC] + [HBM_SPEC] * (len(args) - 1),
        out_specs=(VMEM_SPEC,) * (2 if high > 1 else 1),
        scratch_shapes=[
            pltpu.VMEM((height, wide), jnp.float32),
            pltpu.VMEM((count, height, wide), jnp.float32),
            pltpu.VMEM((count, wide, wide), jnp.float32),
            pltpu.VMEM((2, high, NB, wide // 2), jnp.float32),
            pltpu.SemaphoreType.DMA((count, rows_n + 1)),
            pltpu.SemaphoreType.DMA((2,)),
        ],
        compiler_params=pltpu.CompilerParams(vmem_limit_bytes=LIMIT),
        cost_estimate=cost(2 * height * wide * wide * count * 2),
        name="update",
    )(*args)


def pick_kernel(cuts, me_ref, one_ref, two_ref, *refs):
    sem = refs[-1]
    for which, ref in ((0, two_ref), (1, one_ref)):
        @pl.when(me_ref[1] == which)
        def _(ref=ref):
            copies = [pltpu.make_async_copy(ref.at[pl.ds(lo, dst.shape[0]), :, pl.ds(col, dst.shape[2])], dst, sem.at[i])
                      for i, ((lo, col), dst) in enumerate(zip(cuts, refs[:-1]))]
            for copy in copies:
                copy.start()
            for copy in copies:
                copy.wait()


def pick(me, mats, cuts, width):
    rows = mats[0].shape[0]
    return pl.pallas_call(
        functools.partial(pick_kernel, cuts),
        out_shape=tuple(shape_of(rows - lo, NB, width) for lo, _ in cuts),
        in_specs=[SMEM_SPEC, HBM_SPEC, HBM_SPEC],
        out_specs=(VMEM_SPEC,) * len(cuts),
        scratch_shapes=[pltpu.SemaphoreType.DMA((len(cuts),))],
        compiler_params=pltpu.CompilerParams(vmem_limit_bytes=LIMIT),
        name="pick",
    )(me, *mats)


def place_kernel(steps, *refs):
    me_ref = refs[0]
    kept_refs, got_refs = refs[1:1 + steps], refs[1 + steps:1 + 2 * steps]
    one_ref, two_ref, sem = refs[1 + 2 * steps:]
    now, col = pl.program_id(0), me_ref[1]
    for i in range(steps):
        for which, dst_kept, dst_got in ((0, one_ref, two_ref), (1, two_ref, one_ref)):
            @pl.when(jnp.logical_and(now == i, col == which))
            def _(i=i, dst_kept=dst_kept, dst_got=dst_got):
                rows = pl.ds(i * NB, (steps - i) * NB)
                copies = [pltpu.make_async_copy(kept_refs[i], dst_kept.at[rows, :], sem.at[0]),
                          pltpu.make_async_copy(got_refs[i], dst_got.at[rows, :], sem.at[1])]
                for copy in copies:
                    copy.start()
                if i:
                    dst_kept[:i * NB, :] = jnp.zeros((i * NB, dst_kept.shape[1]), jnp.float32)
                    dst_got[:i * NB, :] = jnp.zeros((i * NB, dst_got.shape[1]), jnp.float32)
                for copy in copies:
                    copy.wait()


def place(me, kept, got):
    steps = len(kept)
    half = kept[0].shape[1]
    spec = pl.BlockSpec((steps * NB, half), lambda i: (0, i))
    return pl.pallas_call(
        functools.partial(place_kernel, steps),
        grid=(steps,),
        out_shape=(shape_of(steps * NB, steps * half),) * 2,
        in_specs=[SMEM_SPEC] + [HBM_SPEC] * (2 * steps),
        out_specs=(spec, spec),
        scratch_shapes=[pltpu.SemaphoreType.DMA((2,))],
        name="place",
    )(me, *kept, *got)


def tie(first, second):
    return lax.optimization_barrier((first, second))


def factor_pair(mat_one, mat_two, rows_n, cols_n):
    row_blocks, _, _ = mat_one.shape
    steps = row_blocks
    wide = rows_n * NB
    half = wide // cols_n
    per = half // NB
    my_row = lax.axis_index("row")
    my_col = lax.axis_index("col")
    first = my_col == 0
    me = jnp.stack([my_row, my_col]).astype(jnp.int32)
    swap = [(0, 1), (1, 0)]

    def hop(value, mask):
        return lax.ppermute(value, "row", [(i, i ^ mask) for i in range(rows_n)])

    def gather(value):
        return [value] + [hop(value, k) for k in range(1, rows_n)]

    def over_col(value):
        return lax.ppermute(value, "col", swap)

    def swapped(step, row_lo, after=None):
        cols = slice(step * half, (step + 1) * half)
        mask = first if after is None else tie(after, first)[1]
        return over_col(jnp.where(mask, mat_two[row_lo:, :, cols], mat_one[row_lo:, :, cols]))

    def panel_of(step, row_lo, row_hi, after=None, ready=None):
        cols = slice(step * half, (step + 1) * half)
        piece_one, piece_two = mat_one[row_lo:row_hi, :, cols], mat_two[row_lo:row_hi, :, cols]
        mask = first if after is None else tie(after, first)[1]
        got = over_col(jnp.where(mask, piece_two, piece_one)) if ready is None else over_col(ready)
        parts = []
        for q in range(per):
            cut = slice(q * NB, (q + 1) * NB)
            mine = jnp.where(first, piece_one[..., cut], piece_two[..., cut])
            parts += [jnp.where(first, mine, got[..., cut]), jnp.where(first, got[..., cut], mine)]
        return jnp.concatenate(parts, axis=-1).reshape(-1, wide), got

    def in_order(rel):
        picked = []
        for q in range(rows_n):
            value = rel[rows_n - 1]
            for k in range(rows_n - 1):
                value = jnp.where(my_row == (q ^ k), rel[k], value)
            picked.append(value)
        return jnp.concatenate(picked, axis=0)

    top, top_got = panel_of(0, 0, 1)
    chain_args = (in_order(gather(top)),)
    sub_own, _ = panel_of(0, 1, 2, top_got)
    diag_own, _ = panel_of(1, 1, 2, top_got)
    _, me_early = tie(top_got, me)
    low_send, rest_send = pick(me_early, (mat_one, mat_two), ((2, 0), (2, half)), half)
    low_own, _ = panel_of(0, 2, steps, ready=low_send)
    rest_own, _ = panel_of(1, 2, steps, ready=rest_send)
    own = jnp.concatenate([sub_own, low_own], axis=0)
    sub_rel, sub_lo = gather(sub_own), 0
    swaps = {}
    lowns, near, later, waiting = [], [], [], {}
    kept, sent = [], []

    for step in range(steps):
        lss, inv = chain(*chain_args)
        for ask in (2, 3) if step == 0 else (step + 3,):
            if ask < steps:
                swaps[ask] = swapped(ask, ask, lss)
        if step >= 2:
            lss, sent[step - 2] = tie(lss, sent[step - 2])
        if step - 2 in waiting:
            lss, far = tie(lss, waiting[step - 2])
            later[step - 2] = [later[step - 2][0], later[step - 2][1], far, hop(far, 1)]
        if step == steps - 1:
            full = lax.dynamic_slice(lss, (my_row * NB, 0), (NB, wide)).reshape(NB, per, cols_n, NB)
            even, odd = full[:, :, 0].reshape(NB, half), full[:, :, 1].reshape(NB, half)
            kept.append(jnp.where(first, even, odd))
            sent.append(lax.ppermute(jnp.where(first, odd, even), "col", swap))
            break
        target = step + 1
        if step >= 1:
            lefts, rights, terms_diag = [], [], []
            for past in range(step):
                base = (target - past - 1) * NB
                lefts.append(lowns[past])
                if past == step - 1:
                    rights.append(near[past])
                    los = (0,) * rows_n
                else:
                    rights.append(later[past])
                    los = ((target - past - 3) * NB,) * rows_n
                terms_diag.append((base, los))
            got = swaps[target]
            lss, me_now = tie(lss, me)
            parts = update(me_now, (mat_one, mat_two), got, target, target, steps - target, lefts, rights, terms_diag)
            diag_own, rest_own = parts if len(parts) > 1 else (parts[0], None)
        next_rel = gather(diag_own)
        if step - 1 < len(later) and step >= 1:
            _, value = tie(diag_own, later[step - 1])
            waiting[step - 1] = hop(value, 2)
            later[step - 1] = [value, hop(value, 1)]
        res = solve(me, lss, inv, own, sub_rel, sub_lo, rest_own)
        lown, chain_args = res[0], (me, res[1], *next_rel)
        lowns.append(lown)
        kept.append(res[2])
        sent.append(over_col(res[3]))
        if rest_own is not None:
            own = res[4]
            near.append(gather(res[5]))
            sub_rel, sub_lo = near[-1], NB
        if len(res) > 6:
            later.append(res[6])
    out_one, out_two = place(me, kept, sent)
    return out_one.reshape(mat_one.shape), out_two.reshape(mat_two.shape)


def solution(mesh):
    rows_n = mesh.shape["row"]
    cols_n = mesh.shape["col"]
    block_spec = P(("part", "row"), None, "col")

    def run_pair(mat_one, mat_two):
        return factor_pair(mat_one, mat_two, rows_n, cols_n)

    return jax.shard_map(run_pair, mesh=mesh, in_specs=(block_spec, block_spec), out_specs=(block_spec, block_spec), check_vma=False)
```

time: 1040 us -> 925 us (0.89)
  local copies, waits for them, and re-layouts: 182 us -> 22 us
  waiting for transfers between devices: 159 us -> 258 us
  other arithmetic: 90.1 us -> 29.9 us
    ppermute x102 -> x78, waiting for transfers between devices: 80.8 us -> 195 us  [hop(): return lax.ppermute(value, 'row', [(i, i ^ mask) for i in range(rows_n)])]
    slice x55 -> x0, local copies, waits for them, and re-layouts: 83.2 us -> none  [the longest x8 22.9 us: emit(): even, odd = (full[:, :, 0], full[:, :, 1])]
    select_n x37 -> x16, other arithmetic: 54.1 us -> 23.4 us  [the longest x8 14.9 us: swapped(): jnp.where(mask, mat_two[row_lo:, :, cols], mat_one[row_lo:, :, cols])]
    concatenate x19 -> x3, other arithmetic: 29.9 us -> 3.23 us  [the longest x2 1.62 us: panel_of(): return (jnp.concatenate(parts, axis=-1).reshape(-1, wide), got)]
    select_n x20 -> x2, local copies, waits for them, and re-layouts: 26.9 us -> 0.84 us  [the longest x1 0.74 us: factor_pair(): kept.append(jnp.where(first, even, odd))]
    reshape x9 -> x0, local copies, waits for them, and re-layouts: 22.9 us -> none  [emit(): full = full.reshape(-1, per, cols_n, NB)]
    pallas_call x10, Pallas kernels: 255 us -> 275 us  [chain(): pl.pallas_call(chain_kernel, out_shape=(shape_of(n, n), shape_of(n, NB)),...]
    unnamed x176 -> x174, local copies, waits for them, and re-layouts: 34.9 us -> 19.9 us
  transfers between devices with their start and end apart: 125 -> 101, of which waited for: 19 -> 31; matrix products, arithmetic and copies ran while one was open for 24% -> 3% of each run, Pallas kernels for 48% -> 49%
where the time goes in v2:
time: 925 us; the launch traced here: 920 us
  Pallas kernels  533 us (58%)
  waiting for transfers between devices  258 us (28%)
  starting transfers between devices  74.2 us (8%)
  other arithmetic  29.9 us (3%)
  local copies, waits for them, and re-layouts  22 us (2%)
    pallas_call x10, Pallas kernels, chain(): pl.pallas_call(chain_kernel, out_shape=(shape_of(n, n), shape_of(n, NB)),...  275 us
    ppermute x78, waiting for transfers between devices, hop(): return lax.ppermute(value, 'row', [(i, i ^ mask) for i in range(rows_n)])  195 us
    pallas_call x9, Pallas kernels, solve(): pl.pallas_call(functools.partial(solve_kernel, rows_n, ahead, far, sub_lo...  124 us
    pallas_call x8, Pallas kernels, update(): pl.pallas_call(functools.partial(update_kernel, rows_n, target, first_row...  108 us
    ppermute x22, waiting for transfers between devices, over_col(): return lax.ppermute(value, 'col', swap)  60 us
    ppermute x78, starting transfers between devices, hop(): return lax.ppermute(value, 'row', [(i, i ^ mask) for i in range(rows_n)])  45.8 us
    ppermute x22, starting transfers between devices, over_col(): return lax.ppermute(value, 'col', swap)  26.9 us
    pallas_call x1, Pallas kernels, place(): pl.pallas_call(functools.partial(place_kernel, steps), grid=(steps,), out...  22.7 us
  transfers between devices with their start and end apart: 101, of which 31 were waited for; matrix products, arithmetic and copies ran while one was open for 3% of the time, Pallas kernels for 49%

profile of v2, /device:TPU:0, one launch (start us, length us, event | category | flops | bytes accessed | tf_op | source)
XLA Modules:
  0.0 919.5 jit_solution(5083837811670093335)
XLA Ops:
  28.8 25.6 %chain.10 = (f32[512,512]{1,0:T(8,128)}, f32[512,128]{1,0:T(8,128)}) custom-call(f32[512,512]{1,0:T(8,128)} %pad_maximum_fusion.3.refs_0_), custom_call_target="tpu_custom_call" | custom-call | flops 2500000000 | bytes 1048576 | tf_op jit(solution)/shard_map/chain/pallas_call | solution.py:111
  61.4 5.0 collective-permute-done.9
  73.5 20.0 %solve.9 = (f32[1152,512]{1,0:T(8,128)}, f32[512,512]{1,0:T(8,128)}, f32[1280,256]{1,0:T(8,128)}, f32[1280,256]{1,0:T(8,128)}, f32[1024,512]{1,0:T(8,128)}, /*index=5*/f32[256,512]{1,0:T(8,128)}, f32[896,512]{1,0:T(8,128)}) custom-call(s32[2]{0:T(128)} %pad_add_fusion.me_ref.refs_0_, f32[512,512]{1,0:T(8,128)} %get-tuple-element.158.refs_1_, ...), custom_call_target="tpu_custom_call" | custom-call | flops 1610612736 | bytes 1048576 | tf_op jit(solution)/shard_map/solve/pallas_call | solution.py:181
  98.2 27.6 %chain.11 = (f32[512,512]{1,0:T(8,128)}, f32[512,128]{1,0:T(8,128)}) custom-call(s32[2]{0:T(128)} %pad_add_fusion.me_ref.refs_0_, f32[512,512]{1,0:T(8,128)} %get-tuple-element.165.refs_1_, f32[128,512]{1,0:T(8,128)} %maximum_bitcast_fusion.2.refs_2_, f32[128,512]{1,0:T(8,128)} %copy-done.86, f32[128,512]{1,0:T(8,128)} %copy-done.67, f32[128,512]{1,0:T(8,128)} %copy-done.64), custom_call_target="tpu_custom_call" | custom-call | flops 2500000000 | bytes 1048576 | tf_op jit(solution)/shard_map/chain/pallas_call | solution.py:111
  127.5 8.3 update.8
  138.8 18.5 %solve.10 = (f32[1024,512]{1,0:T(8,128)}, f32[512,512]{1,0:T(8,128)}, f32[1152,256]{1,0:T(8,128)}, f32[1152,256]{1,0:T(8,128)}, f32[896,512]{1,0:T(8,128)}, /*index=5*/f32[256,512]{1,0:T(8,128)}, f32[768,512]{1,0:T(8,128)}) custom-call(s32[2]{0:T(128)} %pad_add_fusion.me_ref.refs_0_, f32[512,512]{1,0:T(8,128)} %get-tuple-element.167.refs_1_, ...), custom_call_target="tpu_custom_call" | custom-call | flops 1476395008 | bytes 1048576 | tf_op jit(solution)/shard_map/solve/pallas_call | solution.py:181
  157.4 25.9 %collective-permute-done.20.refs_5_ = f32[128,512]{1,0:T(8,128)S(1)} collective-permute-done((f32[128,512]{1,0:T(8,128)}, f32[128,512]{1,0:T(8,128)S(1)}, u32[]{:S(2)}, u32[]{:S(2)}) %collective-permute-start.20) | collective-permute-done | bytes 262176 | tf_op jit(solution)/shard_map/ppermute | solution.py:341
  184.3 5.3 collective-permute-done.19.refs_4_
  189.6 27.8 %chain.12 = (f32[512,512]{1,0:T(8,128)}, f32[512,128]{1,0:T(8,128)}) custom-call(s32[2]{0:T(128)} %pad_add_fusion.me_ref.refs_0_, f32[512,512]{1,0:T(8,128)} %get-tuple-element.176.refs_1_, f32[128,512]{1,0:T(8,128)} %get-tuple-element.177.refs_2_, f32[128,512]{1,0:T(8,128)} %collective-permute-done.18.refs_3_, f32[128,512]{1,0:T(8,128)} %collective-permute-done.19.refs_4_, ...), custom_call_target="tpu_custom_call" | custom-call | flops 2500000000 | bytes 1048576 | tf_op jit(solution)/shard_map/chain/pallas_call | solution.py:111
  221.5 20.4 %collective-permute-done.26.refs_3_ = f32[7,128,256]{2,1,0:T(8,128)S(1)} collective-permute-done((f32[7,128,256]{2,1,0:T(8,128)S(1)}, f32[7,128,256]{2,1,0:T(8,128)S(1)}, u32[]{:S(2)}, u32[]{:S(2)}) %collective-permute-start.26) | collective-permute-done | bytes 917536 | tf_op jit(solution)/shard_map/ppermute | solution.py:347
  246.4 11.6 %update.9 = (f32[128,512]{1,0:T(8,128)}, f32[768,512]{1,0:T(8,128)}) custom-call(s32[2]{0:T(128)} %pad_add_fusion.me_ref.refs_0_, f32[10,128,2560]{2,1,0:T(8,128)} %refs_1_.15, f32[10,128,2560]{2,1,0:T(8,128)} %refs_2_.15, f32[7,128,256]{2,1,0:T(8,128)} %copy-done.49, f32[1152,512]{1,0:T(8,128)} %get-tuple-element.173.refs_4_, ...), custom_call_target="tpu_custom_call" | custom-call | flops 1879048192 | bytes 1048576 | tf_op jit(solution)/shard_map/update/pallas_call | solution.py:243
  262.1 16.8 %solve.11 = (f32[896,512]{1,0:T(8,128)}, f32[512,512]{1,0:T(8,128)}, f32[1024,256]{1,0:T(8,128)}, f32[1024,256]{1,0:T(8,128)}, f32[768,512]{1,0:T(8,128)}, /*index=5*/f32[256,512]{1,0:T(8,128)}, f32[640,512]{1,0:T(8,128)}) custom-call(s32[2]{0:T(128)} %pad_add_fusion.me_ref.refs_0_, f32[512,512]{1,0:T(8,128)} %get-tuple-element.184.refs_1_, ...), custom_call_target="tpu_custom_call" | custom-call | flops 1342177280 | bytes 1048576 | tf_op jit(solution)/shard_map/solve/pallas_call | solution.py:181
  279.0 20.2 %collective-permute-done.31.refs_5_ = f32[128,512]{1,0:T(8,128)S(1)} collective-permute-done((f32[128,512]{1,0:T(8,128)}, f32[128,512]{1,0:T(8,128)S(1)}, u32[]{:S(2)}, u32[]{:S(2)}) %collective-permute-start.31) | collective-permute-done | bytes 262176 | tf_op jit(solution)/shard_map/ppermute | solution.py:341
  300.7 5.0 collective-permute-done.30.refs_4_
  305.7 27.6 %chain.13 = (f32[512,512]{1,0:T(8,128)}, f32[512,128]{1,0:T(8,128)}) custom-call(s32[2]{0:T(128)} %pad_add_fusion.me_ref.refs_0_, f32[512,512]{1,0:T(8,128)} %get-tuple-element.193.refs_1_, f32[128,512]{1,0:T(8,128)} %get-tuple-element.194.refs_2_, f32[128,512]{1,0:T(8,128)} %collective-permute-done.29.refs_3_, f32[128,512]{1,0:T(8,128)} %collective-permute-done.30.refs_4_, ...), custom_call_target="tpu_custom_call" | custom-call | flops 2500000000 | bytes 1048576 | tf_op jit(solution)/shard_map/chain/pallas_call | solution.py:111
  338.3 16.7 %collective-permute-done.37.refs_3_ = f32[6,128,256]{2,1,0:T(8,128)} collective-permute-done((f32[6,128,256]{2,1,0:T(8,128)S(1)}, f32[6,128,256]{2,1,0:T(8,128)}, u32[]{:S(2)}, u32[]{:S(2)}) %collective-permute-start.37) | collective-permute-done | bytes 786464 | tf_op jit(solution)/shard_map/ppermute | solution.py:347
  355.0 7.1 collective-permute-done.35.refs_17_.refs_5_
  364.4 14.0 %update.10 = (f32[128,512]{1,0:T(8,128)}, f32[640,512]{1,0:T(8,128)}) custom-call(s32[2]{0:T(128)} %pad_add_fusion.me_ref.refs_0_, f32[10,128,2560]{2,1,0:T(8,128)} %refs_1_.15, f32[10,128,2560]{2,1,0:T(8,128)} %refs_2_.15, f32[6,128,256]{2,1,0:T(8,128)} %collective-permute-done.37.refs_3_, f32[1152,512]{1,0:T(8,128)} %get-tuple-element.173.refs_4_, ...), custom_call_target="tpu_custom_call" | custom-call | flops 2415919104 | bytes 1048576 | tf_op jit(solution)/shard_map/update/pallas_call | solution.py:243
  381.5 15.5 %solve.12 = (f32[768,512]{1,0:T(8,128)}, f32[512,512]{1,0:T(8,128)}, f32[896,256]{1,0:T(8,128)}, f32[896,256]{1,0:T(8,128)}, f32[640,512]{1,0:T(8,128)}, /*index=5*/f32[256,512]{1,0:T(8,128)}, f32[512,512]{1,0:T(8,128)}) custom-call(s32[2]{0:T(128)} %pad_add_fusion.me_ref.refs_0_, f32[512,512]{1,0:T(8,128)} %get-tuple-element.201.refs_1_, ...), custom_call_target="tpu_custom_call" | custom-call | flops 1207959552 | bytes 1048576 | tf_op jit(solution)/shard_map/solve/pallas_call | solution.py:181
  397.1 17.0 %collective-permute-done.42.refs_5_ = f32[128,512]{1,0:T(8,128)S(1)} collective-permute-done((f32[128,512]{1,0:T(8,128)}, f32[128,512]{1,0:T(8,128)S(1)}, u32[]{:S(2)}, u32[]{:S(2)}) %collective-permute-start.42) | collective-permute-done | bytes 262176 | tf_op jit(solution)/shard_map/ppermute | solution.py:341
  415.5 4.9 collective-permute-done.41.refs_4_
  421.9 27.6 %chain.14 = (f32[512,512]{1,0:T(8,128)}, f32[512,128]{1,0:T(8,128)}) custom-call(s32[2]{0:T(128)} %pad_add_fusion.me_ref.refs_0_, f32[512,512]{1,0:T(8,128)} %get-tuple-element.211.refs_1_, f32[128,512]{1,0:T(8,128)} %get-tuple-element.212.refs_2_, f32[128,512]{1,0:T(8,128)} %copy-done.85, f32[128,512]{1,0:T(8,128)} %copy-done.84, f32[128,512]{1,0:T(8,128)} %copy-done.81), custom_call_target="tpu_custom_call" | custom-call | flops 2500000000 | bytes 1048576 | tf_op jit(solution)/shard_map/chain/pallas_call | solution.py:111
  453.2 15.0 %collective-permute-done.48.refs_3_ = f32[5,128,256]{2,1,0:T(8,128)} collective-permute-done((f32[5,128,256]{2,1,0:T(8,128)S(1)}, f32[5,128,256]{2,1,0:T(8,128)}, u32[]{:S(2)}, u32[]{:S(2)}) %collective-permute-start.48) | collective-permute-done | bytes 655392 | tf_op jit(solution)/shard_map/ppermute | solution.py:347
  468.2 8.9 collective-permute-done.46.refs_22_.refs_5_
  479.3 15.2 %update.11 = (f32[128,512]{1,0:T(8,128)}, f32[512,512]{1,0:T(8,128)}) custom-call(s32[2]{0:T(128)} %pad_add_fusion.me_ref.refs_0_, f32[10,128,2560]{2,1,0:T(8,128)} %refs_1_.15, f32[10,128,2560]{2,1,0:T(8,128)} %refs_2_.15, f32[5,128,256]{2,1,0:T(8,128)} %collective-permute-done.48.refs_3_, f32[1152,512]{1,0:T(8,128)} %get-tuple-element.173.refs_4_, ...), custom_call_target="tpu_custom_call" | custom-call | flops 2684354560 | bytes 1048576 | tf_op jit(solution)/shard_map/update/pallas_call | solution.py:243
  500.9 13.8 %solve.13 = (f32[640,512]{1,0:T(8,128)}, f32[512,512]{1,0:T(8,128)}, f32[768,256]{1,0:T(8,128)}, f32[768,256]{1,0:T(8,128)}, f32[512,512]{1,0:T(8,128)}, /*index=5*/f32[256,512]{1,0:T(8,128)}, f32[384,512]{1,0:T(8,128)}) custom-call(s32[2]{0:T(128)} %pad_add_fusion.me_ref.refs_0_, f32[512,512]{1,0:T(8,128)} %get-tuple-element.219.refs_1_, ...), custom_call_target="tpu_custom_call" | custom-call | flops 1073741824 | bytes 1048576 | tf_op jit(solution)/shard_map/solve/pallas_call | solution.py:181
  514.8 9.8 %collective-permute-done.53.refs_5_ = f32[128,512]{1,0:T(8,128)S(1)} collective-permute-done((f32[128,512]{1,0:T(8,128)}, f32[128,512]{1,0:T(8,128)S(1)}, u32[]{:S(2)}, u32[]{:S(2)}) %collective-permute-start.53) | collective-permute-done | bytes 262176 | tf_op jit(solution)/shard_map/ppermute | solution.py:341
  532.3 27.8 %chain.15 = (f32[512,512]{1,0:T(8,128)}, f32[512,128]{1,0:T(8,128)}) custom-call(s32[2]{0:T(128)} %pad_add_fusion.me_ref.refs_0_, f32[512,512]{1,0:T(8,128)} %get-tuple-element.229.refs_1_, f32[128,512]{1,0:T(8,128)} %get-tuple-element.230.refs_2_, f32[128,512]{1,0:T(8,128)} %copy-done.82, f32[128,512]{1,0:T(8,128)} %copy-done.77, f32[128,512]{1,0:T(8,128)} %copy-done.74), custom_call_target="tpu_custom_call" | custom-call | flops 2500000000 | bytes 1048576 | tf_op jit(solution)/shard_map/chain/pallas_call | solution.py:111
  562.3 11.7 %collective-permute-done.58.refs_28_.refs_6_ = f32[256,512]{1,0:T(8,128)S(1)} collective-permute-done((f32[256,512]{1,0:T(8,128)}, f32[256,512]{1,0:T(8,128)S(1)}, u32[]{:S(2)}, u32[]{:S(2)}) %collective-permute-start.58) | collective-permute-done | bytes 524320 | tf_op jit(solution)/shard_map/ppermute | solution.py:341
  575.7 10.2 %collective-permute-done.57.refs_27_.refs_5_ = f32[256,512]{1,0:T(8,128)S(1)} collective-permute-done((f32[256,512]{1,0:T(8,128)}, f32[256,512]{1,0:T(8,128)S(1)}, u32[]{:S(2)}, u32[]{:S(2)}) %collective-permute-start.57) | collective-permute-done | bytes 524320 | tf_op jit(solution)/shard_map/ppermute | solution.py:341
  587.9 15.6 %update.12 = (f32[128,512]{1,0:T(8,128)}, f32[384,512]{1,0:T(8,128)}) custom-call(s32[2]{0:T(128)} %pad_add_fusion.me_ref.refs_0_, f32[10,128,2560]{2,1,0:T(8,128)} %refs_1_.15, f32[10,128,2560]{2,1,0:T(8,128)} %refs_2_.15, f32[4,128,256]{2,1,0:T(8,128)} %collective-permute-done.59.refs_3_, f32[1152,512]{1,0:T(8,128)} %get-tuple-element.173.refs_4_, ...), custom_call_target="tpu_custom_call" | custom-call | flops 2684354560 | bytes 1048576 | tf_op jit(solution)/shard_map/update/pallas_call | solution.py:243
  608.1 12.1 %solve.14 = (f32[512,512]{1,0:T(8,128)}, f32[512,512]{1,0:T(8,128)}, f32[640,256]{1,0:T(8,128)}, f32[640,256]{1,0:T(8,128)}, f32[384,512]{1,0:T(8,128)}, /*index=5*/f32[256,512]{1,0:T(8,128)}, f32[256,512]{1,0:T(8,128)}) custom-call(s32[2]{0:T(128)} %pad_add_fusion.me_ref.refs_0_, f32[512,512]{1,0:T(8,128)} %get-tuple-element.237.refs_1_, ...), custom_call_target="tpu_custom_call" | custom-call | flops 939524096 | bytes 1048576 | tf_op jit(solution)/shard_map/solve/pallas_call | solution.py:181
  620.2 7.7 collective-permute-done.64.refs_5_
  634.6 27.6 %chain.16 = (f32[512,512]{1,0:T(8,128)}, f32[512,128]{1,0:T(8,128)}) custom-call(s32[2]{0:T(128)} %pad_add_fusion.me_ref.refs_0_, f32[512,512]{1,0:T(8,128)} %get-tuple-element.247.refs_1_, f32[128,512]{1,0:T(8,128)} %get-tuple-element.248.refs_2_, f32[128,512]{1,0:T(8,128)} %copy-done.83, f32[128,512]{1,0:T(8,128)} %copy-done.78, f32[128,512]{1,0:T(8,128)} %copy-done.75), custom_call_target="tpu_custom_call" | custom-call | flops 2500000000 | bytes 1048576 | tf_op jit(solution)/shard_map/chain/pallas_call | solution.py:111
  664.6 12.3 %collective-permute-done.69.refs_33_.refs_6_ = f32[256,512]{1,0:T(8,128)S(1)} collective-permute-done((f32[256,512]{1,0:T(8,128)}, f32[256,512]{1,0:T(8,128)S(1)}, u32[]{:S(2)}, u32[]{:S(2)}) %collective-permute-start.69) | collective-permute-done | bytes 524320 | tf_op jit(solution)/shard_map/ppermute | solution.py:341
  678.5 9.9 %collective-permute-done.68.refs_32_.refs_5_ = f32[256,512]{1,0:T(8,128)S(1)} collective-permute-done((f32[256,512]{1,0:T(8,128)}, f32[256,512]{1,0:T(8,128)S(1)}, u32[]{:S(2)}, u32[]{:S(2)}) %collective-permute-start.68) | collective-permute-done | bytes 524320 | tf_op jit(solution)/shard_map/ppermute | solution.py:341
  690.2 14.8 %update.13 = (f32[128,512]{1,0:T(8,128)}, f32[256,512]{1,0:T(8,128)}) custom-call(s32[2]{0:T(128)} %pad_add_fusion.me_ref.refs_0_, f32[10,128,2560]{2,1,0:T(8,128)} %refs_1_.15, f32[10,128,2560]{2,1,0:T(8,128)} %refs_2_.15, f32[3,128,256]{2,1,0:T(8,128)} %copy-done.50, f32[1152,512]{1,0:T(8,128)} %get-tuple-element.173.refs_4_, ...), custom_call_target="tpu_custom_call" | custom-call | flops 2415919104 | bytes 1048576 | tf_op jit(solution)/shard_map/update/pallas_call | solution.py:243
  708.8 5.0 collective-permute-done.75.refs_5_
  715.4 10.9 %solve.15 = (f32[384,512]{1,0:T(8,128)}, f32[512,512]{1,0:T(8,128)}, f32[512,256]{1,0:T(8,128)}, f32[512,256]{1,0:T(8,128)}, f32[256,512]{1,0:T(8,128)}, /*index=5*/f32[256,512]{1,0:T(8,128)}, f32[128,512]{1,0:T(8,128)}) custom-call(s32[2]{0:T(128)} %pad_add_fusion.me_ref.refs_0_, f32[512,512]{1,0:T(8,128)} %get-tuple-element.255.refs_1_, ...), custom_call_target="tpu_custom_call" | custom-call | flops 805306368 | bytes 1048576 | tf_op jit(solution)/shard_map/solve/pallas_call | solution.py:181
  727.3 27.6 %chain.17 = (f32[512,512]{1,0:T(8,128)}, f32[512,128]{1,0:T(8,128)}) custom-call(s32[2]{0:T(128)} %pad_add_fusion.me_ref.refs_0_, f32[512,512]{1,0:T(8,128)} %get-tuple-element.265.refs_1_, f32[128,512]{1,0:T(8,128)} %get-tuple-element.266.refs_2_, f32[128,512]{1,0:T(8,128)} %copy-done.72, f32[128,512]{1,0:T(8,128)} %copy-done.70, f32[128,512]{1,0:T(8,128)} %copy-done.69), custom_call_target="tpu_custom_call" | custom-call | flops 2500000000 | bytes 1048576 | tf_op jit(solution)/shard_map/chain/pallas_call | solution.py:111
  757.1 12.0 %collective-permute-done.79.refs_37_.refs_5_ = f32[256,512]{1,0:T(8,128)S(1)} collective-permute-done((f32[256,512]{1,0:T(8,128)S(1)}, f32[256,512]{1,0:T(8,128)S(1)}, u32[]{:S(2)}, u32[]{:S(2)}) %collective-permute-start.79) | collective-permute-done | bytes 524320 | tf_op jit(solution)/shard_map/ppermute | solution.py:341
  770.3 13.4 %update.14 = (f32[128,512]{1,0:T(8,128)}, f32[128,512]{1,0:T(8,128)}) custom-call(s32[2]{0:T(128)} %pad_add_fusion.me_ref.refs_0_, f32[10,128,2560]{2,1,0:T(8,128)} %refs_1_.15, f32[10,128,2560]{2,1,0:T(8,128)} %refs_2_.15, f32[2,128,256]{2,1,0:T(8,128)} %copy-done.53, f32[1152,512]{1,0:T(8,128)} %get-tuple-element.173.refs_4_, ...), custom_call_target="tpu_custom_call" | custom-call | flops 1879048192 | bytes 1048576 | tf_op jit(solution)/shard_map/update/pallas_call | solution.py:243
  785.6 9.2 solve.16
  800.1 27.6 %chain.18 = (f32[512,512]{1,0:T(8,128)}, f32[512,128]{1,0:T(8,128)}) custom-call(s32[2]{0:T(128)} %pad_add_fusion.me_ref.refs_0_, f32[512,512]{1,0:T(8,128)} %get-tuple-element.283.refs_1_, f32[128,512]{1,0:T(8,128)} %get-tuple-element.284.refs_2_, f32[128,512]{1,0:T(8,128)} %copy-done.68, f32[128,512]{1,0:T(8,128)} %copy-done.66, f32[128,512]{1,0:T(8,128)} %copy-done.65), custom_call_target="tpu_custom_call" | custom-call | flops 2500000000 | bytes 1048576 | tf_op jit(solution)/shard_map/chain/pallas_call | solution.py:111
  830.9 15.2 %update.15.refs_2_ = f32[128,512]{1,0:T(8,128)} custom-call(s32[2]{0:T(128)} %pad_add_fusion.me_ref.refs_0_, f32[10,128,2560]{2,1,0:T(8,128)} %refs_1_.15, f32[10,128,2560]{2,1,0:T(8,128)} %refs_2_.15, f32[1,128,256]{2,1,0:T(8,128)} %copy-done.61, f32[1152,512]{1,0:T(8,128)} %get-tuple-element.173.refs_4_, f32[1024,512]{1,0:T(8,128)} %get-tuple-element.189.refs_5_, ...), custom_call_target="tpu_custom_call" | custom-call | flops 1073741824 | bytes 1048576 | tf_op jit(solution)/shard_map/update/pallas_call | solution.py:243
  849.4 7.4 solve.17
  861.4 27.7 %chain.19 = (f32[512,512]{1,0:T(8,128)}, f32[512,128]{1,0:T(8,128)}) custom-call(s32[2]{0:T(128)} %pad_add_fusion.me_ref.refs_0_, f32[512,512]{1,0:T(8,128)} %get-tuple-element.295.refs_1_, f32[128,512]{1,0:T(8,128)} %update.15.refs_2_, f32[128,512]{1,0:T(8,128)} %copy-done.76, f32[128,512]{1,0:T(8,128)} %copy-done.73, f32[128,512]{1,0:T(8,128)} %copy-done.71), custom_call_target="tpu_custom_call" | custom-call | flops 2500000000 | bytes 1048576 | tf_op jit(solution)/shard_map/chain/pallas_call | solution.py:111
  896.3 22.7 %place.1 = (f32[1280,2560]{1,0:T(8,128)}, f32[1280,2560]{1,0:T(8,128)}) custom-call(s32[2]{0:T(128)} %pad_add_fusion.me_ref.refs_0_, f32[1280,256]{1,0:T(8,128)} %get-tuple-element.164.refs_1_, f32[1152,256]{1,0:T(8,128)} %get-tuple-element.175.refs_2_, f32[1024,256]{1,0:T(8,128)} %get-tuple-element.192.refs_3_, f32[896,256]{1,0:T(8,128)} %get-tuple-element.210.refs_4_, ...), custom_call_target="tpu_custom_call" | custom-call | tf_op jit(solution)/shard_map/place/pallas_call | solution.py:313
  (387 shorter events, 157.4 us)
Async XLA Ops:
  19.1 38.1 %collective-permute-start.8 = (f32[8,128,256]{2,1,0:T(8,128)}, f32[8,128,256]{2,1,0:T(8,128)S(1)}, u32[]{:S(2)}, u32[]{:S(2)}) collective-permute-start(f32[8,128,256]{2,1,0:T(8,128)} %get-tuple-element.162), channel_id=1, source_target_pairs={{0,4},{4,0},{1,5},{5,1},{2,6},{6,2},{3,7},{7,3}} | collective-permute-start | bytes 3145736 | tf_op jit(solution)/shard_map/ppermute | solution.py:347
  21.8 44.5 %collective-permute-start.9 = (f32[8,128,256]{2,1,0:T(8,128)}, f32[8,128,256]{2,1,0:T(8,128)S(1)}, u32[]{:S(2)}, u32[]{:S(2)}) collective-permute-start(f32[8,128,256]{2,1,0:T(8,128)} %get-tuple-element.163), channel_id=1, source_target_pairs={{0,4},{4,0},{1,5},{5,1},{2,6},{6,2},{3,7},{7,3}} | collective-permute-start | bytes 3145736 | tf_op jit(solution)/shard_map/ppermute | solution.py:347
  23.8 45.9 %collective-permute-start.7 = (f32[128,512]{1,0:T(8,128)S(1)}, f32[128,512]{1,0:T(8,128)S(1)}, u32[]{:S(2)}, u32[]{:S(2)}) collective-permute-start(f32[128,512]{1,0:T(8,128)S(1)} %maximum_bitcast_fusion.1.refs_3_), channel_id=1, source_target_pairs={{0,3},{1,2},{2,1},{3,0},{4,7},{5,6},{6,5},{7,4}} | collective-permute-start | bytes 786440 | tf_op jit(solution)/shard_map/ppermute | solution.py:341
  24.1 48.7 %collective-permute-start.6 = (f32[128,512]{1,0:T(8,128)S(1)}, f32[128,512]{1,0:T(8,128)S(1)}, u32[]{:S(2)}, u32[]{:S(2)}) collective-permute-start(f32[128,512]{1,0:T(8,128)S(1)} %maximum_bitcast_fusion.1.refs_3_), channel_id=1, source_target_pairs={{0,2},{1,3},{2,0},{3,1},{4,6},{5,7},{6,4},{7,5}} | collective-permute-start | bytes 786440 | tf_op jit(solution)/shard_map/ppermute | solution.py:341
  27.5 45.2 %collective-permute-start.5 = (f32[128,512]{1,0:T(8,128)S(1)}, f32[128,512]{1,0:T(8,128)}, u32[]{:S(2)}, u32[]{:S(2)}) collective-permute-start(f32[128,512]{1,0:T(8,128)S(1)} %maximum_bitcast_fusion.1.refs_3_), channel_id=1, source_target_pairs={{0,1},{1,0},{2,3},{3,2},{4,5},{5,4},{6,7},{7,6}} | collective-permute-start | bytes 786440 | tf_op jit(solution)/shard_map/ppermute | solution.py:341
  57.2 36.9 %collective-permute-start.13 = (f32[128,512]{1,0:T(8,128)S(1)}, f32[128,512]{1,0:T(8,128)S(1)}, u32[]{:S(2)}, u32[]{:S(2)}) collective-permute-start(f32[128,512]{1,0:T(8,128)S(1)} %copy-done.60), channel_id=1, source_target_pairs={{0,3},{1,2},{2,1},{3,0},{4,7},{5,6},{6,5},{7,4}} | collective-permute-start | bytes 786440 | tf_op jit(solution)/shard_map/ppermute | solution.py:341
  66.4 59.4 %collective-permute-start.17 = (f32[8,128,256]{2,1,0:T(8,128)}, f32[8,128,256]{2,1,0:T(8,128)S(1)}, u32[]{:S(2)}, u32[]{:S(2)}) collective-permute-start(f32[8,128,256]{2,1,0:T(8,128)} %slice_select_fusion), channel_id=1, source_target_pairs={{0,4},{4,0},{1,5},{5,1},{2,6},{6,2},{3,7},{7,3}} | collective-permute-start | bytes 3145736 | tf_op jit(solution)/shard_map/ppermute | solution.py:347
  93.5 32.3 %collective-permute-start.16 = (f32[256,512]{1,0:T(8,128)}, f32[256,512]{1,0:T(8,128)S(1)}, u32[]{:S(2)}, u32[]{:S(2)}) collective-permute-start(f32[256,512]{1,0:T(8,128)} %get-tuple-element.169.refs_5_.refs_3_), channel_id=1, source_target_pairs={{0,3},{1,2},{2,1},{3,0},{4,7},{5,6},{6,5},{7,4}} | collective-permute-start | bytes 1572872 | tf_op jit(solution)/shard_map/ppermute | solution.py:341
  93.5 32.3 %collective-permute-start.15 = (f32[256,512]{1,0:T(8,128)}, f32[256,512]{1,0:T(8,128)S(1)}, u32[]{:S(2)}, u32[]{:S(2)}) collective-permute-start(f32[256,512]{1,0:T(8,128)} %get-tuple-element.169.refs_5_.refs_3_), channel_id=1, source_target_pairs={{0,2},{1,3},{2,0},{3,1},{4,6},{5,7},{6,4},{7,5}} | collective-permute-start | bytes 1572872 | tf_op jit(solution)/shard_map/ppermute | solution.py:341
  94.0 31.8 %collective-permute-start.14 = (f32[256,512]{1,0:T(8,128)}, f32[256,512]{1,0:T(8,128)S(1)}, u32[]{:S(2)}, u32[]{:S(2)}) collective-permute-start(f32[256,512]{1,0:T(8,128)} %get-tuple-element.169.refs_5_.refs_3_), channel_id=1, source_target_pairs={{0,1},{1,0},{2,3},{3,2},{4,5},{5,4},{6,7},{7,6}} | collective-permute-start | bytes 1572872 | tf_op jit(solution)/shard_map/ppermute | solution.py:341
  135.9 81.5 %collective-permute-start.22 = (f32[896,512]{1,0:T(8,128)S(1)}, f32[896,512]{1,0:T(8,128)}, u32[]{:S(2)}, u32[]{:S(2)}) collective-permute-start(f32[896,512]{1,0:T(8,128)S(1)} %copy-done), channel_id=1, source_target_pairs={{0,2},{1,3},{2,0},{3,1},{4,6},{5,7},{6,4},{7,5}} | collective-permute-start | bytes 5505032 | tf_op jit(solution)/shard_map/ppermute | solution.py:341
  136.5 80.9 %collective-permute-start.21 = (f32[1280,256]{1,0:T(8,128)}, f32[1280,256]{1,0:T(8,128)S(1)}, u32[]{:S(2)}, u32[]{:S(2)}) collective-permute-start(f32[1280,256]{1,0:T(8,128)} %get-tuple-element.179), channel_id=1, source_target_pairs={{0,4},{4,0},{1,5},{5,1},{2,6},{6,2},{3,7},{7,3}} | collective-permute-start | bytes 3932168 | tf_op jit(solution)/shard_map/ppermute | solution.py:347
  137.0 46.3 %collective-permute-start.20 = (f32[128,512]{1,0:T(8,128)}, f32[128,512]{1,0:T(8,128)S(1)}, u32[]{:S(2)}, u32[]{:S(2)}) collective-permute-start(f32[128,512]{1,0:T(8,128)} %get-tuple-element.177.refs_2_), channel_id=1, source_target_pairs={{0,3},{1,2},{2,1},{3,0},{4,7},{5,6},{6,5},{7,4}} | collective-permute-start | bytes 786440 | tf_op jit(solution)/shard_map/ppermute | solution.py:341
  137.9 51.7 %collective-permute-start.19 = (f32[128,512]{1,0:T(8,128)}, f32[128,512]{1,0:T(8,128)}, u32[]{:S(2)}, u32[]{:S(2)}) collective-permute-start(f32[128,512]{1,0:T(8,128)} %get-tuple-element.177.refs_2_), channel_id=1, source_target_pairs={{0,2},{1,3},{2,0},{3,1},{4,6},{5,7},{6,4},{7,5}} | collective-permute-start | bytes 786440 | tf_op jit(solution)/shard_map/ppermute | solution.py:341
  138.4 51.1 %collective-permute-start.18 = (f32[128,512]{1,0:T(8,128)}, f32[128,512]{1,0:T(8,128)}, u32[]{:S(2)}, u32[]{:S(2)}) collective-permute-start(f32[128,512]{1,0:T(8,128)} %get-tuple-element.177.refs_2_), channel_id=1, source_target_pairs={{0,1},{1,0},{2,3},{3,2},{4,5},{5,4},{6,7},{7,6}} | collective-permute-start | bytes 786440 | tf_op jit(solution)/shard_map/ppermute | solution.py:341
  183.2 62.1 %collective-permute-start.27 = (f32[896,512]{1,0:T(8,128)S(1)}, f32[896,512]{1,0:T(8,128)}, u32[]{:S(2)}, u32[]{:S(2)}) collective-permute-start(f32[896,512]{1,0:T(8,128)S(1)} %copy-done), channel_id=1, source_target_pairs={{0,1},{1,0},{2,3},{3,2},{4,5},{5,4},{6,7},{7,6}} | collective-permute-start | bytes 5505032 | tf_op jit(solution)/shard_map/ppermute | solution.py:341
  257.9 75.4 %collective-permute-start.33 = (f32[768,512]{1,0:T(8,128)S(1)}, f32[768,512]{1,0:T(8,128)S(1)}, u32[]{:S(2)}, u32[]{:S(2)}) collective-permute-start(f32[768,512]{1,0:T(8,128)S(1)} %copy-done.1), channel_id=1, source_target_pairs={{0,2},{1,3},{2,0},{3,1},{4,6},{5,7},{6,4},{7,5}} | collective-permute-start | bytes 4718600 | tf_op jit(solution)/shard_map/ppermute | solution.py:341
  258.6 74.8 %collective-permute-start.32 = (f32[1152,256]{1,0:T(8,128)}, f32[1152,256]{1,0:T(8,128)}, u32[]{:S(2)}, u32[]{:S(2)}) collective-permute-start(f32[1152,256]{1,0:T(8,128)} %get-tuple-element.196), channel_id=1, source_target_pairs={{0,4},{4,0},{1,5},{5,1},{2,6},{6,2},{3,7},{7,3}} | collective-permute-start | bytes 3538952 | tf_op jit(solution)/shard_map/ppermute | solution.py:347
  260.3 38.9 %collective-permute-start.31 = (f32[128,512]{1,0:T(8,128)}, f32[128,512]{1,0:T(8,128)S(1)}, u32[]{:S(2)}, u32[]{:S(2)}) collective-permute-start(f32[128,512]{1,0:T(8,128)} %get-tuple-element.194.refs_2_), channel_id=1, source_target_pairs={{0,3},{1,2},{2,1},{3,0},{4,7},{5,6},{6,5},{7,4}} | collective-permute-start | bytes 786440 | tf_op jit(solution)/shard_map/ppermute | solution.py:341
  260.7 45.0 %collective-permute-start.30 = (f32[128,512]{1,0:T(8,128)}, f32[128,512]{1,0:T(8,128)}, u32[]{:S(2)}, u32[]{:S(2)}) collective-permute-start(f32[128,512]{1,0:T(8,128)} %get-tuple-element.194.refs_2_), channel_id=1, source_target_pairs={{0,2},{1,3},{2,0},{3,1},{4,6},{5,7},{6,4},{7,5}} | collective-permute-start | bytes 786440 | tf_op jit(solution)/shard_map/ppermute | solution.py:341
  261.5 44.2 %collective-permute-start.29 = (f32[128,512]{1,0:T(8,128)}, f32[128,512]{1,0:T(8,128)}, u32[]{:S(2)}, u32[]{:S(2)}) collective-permute-start(f32[128,512]{1,0:T(8,128)} %get-tuple-element.194.refs_2_), channel_id=1, source_target_pairs={{0,1},{1,0},{2,3},{3,2},{4,5},{5,4},{6,7},{7,6}} | collective-permute-start | bytes 786440 | tf_op jit(solution)/shard_map/ppermute | solution.py:341
  299.1 63.0 %collective-permute-start.38 = (f32[768,512]{1,0:T(8,128)S(1)}, f32[768,512]{1,0:T(8,128)}, u32[]{:S(2)}, u32[]{:S(2)}) collective-permute-start(f32[768,512]{1,0:T(8,128)S(1)} %copy-done.1), channel_id=1, source_target_pairs={{0,1},{1,0},{2,3},{3,2},{4,5},{5,4},{6,7},{7,6}} | collective-permute-start | bytes 4718600 | tf_op jit(solution)/shard_map/ppermute | solution.py:341
  378.4 71.2 %collective-permute-start.44 = (f32[640,512]{1,0:T(8,128)S(1)}, f32[640,512]{1,0:T(8,128)S(1)}, u32[]{:S(2)}, u32[]{:S(2)}) collective-permute-start(f32[640,512]{1,0:T(8,128)S(1)} %copy-done.4), channel_id=1, source_target_pairs={{0,2},{1,3},{2,0},{3,1},{4,6},{5,7},{6,4},{7,5}} | collective-permute-start | bytes 3932168 | tf_op jit(solution)/shard_map/ppermute | solution.py:341
  379.2 70.3 %collective-permute-start.43 = (f32[1024,256]{1,0:T(8,128)}, f32[1024,256]{1,0:T(8,128)}, u32[]{:S(2)}, u32[]{:S(2)}) collective-permute-start(f32[1024,256]{1,0:T(8,128)} %get-tuple-element.214), channel_id=1, source_target_pairs={{0,4},{4,0},{1,5},{5,1},{2,6},{6,2},{3,7},{7,3}} | collective-permute-start | bytes 3145736 | tf_op jit(solution)/shard_map/ppermute | solution.py:347
  379.7 34.4 %collective-permute-start.42 = (f32[128,512]{1,0:T(8,128)}, f32[128,512]{1,0:T(8,128)S(1)}, u32[]{:S(2)}, u32[]{:S(2)}) collective-permute-start(f32[128,512]{1,0:T(8,128)} %get-tuple-element.212.refs_2_), channel_id=1, source_target_pairs={{0,3},{1,2},{2,1},{3,0},{4,7},{5,6},{6,5},{7,4}} | collective-permute-start | bytes 786440 | tf_op jit(solution)/shard_map/ppermute | solution.py:341
  380.0 40.5 %collective-permute-start.41 = (f32[128,512]{1,0:T(8,128)}, f32[128,512]{1,0:T(8,128)S(1)}, u32[]{:S(2)}, u32[]{:S(2)}) collective-permute-start(f32[128,512]{1,0:T(8,128)} %get-tuple-element.212.refs_2_), channel_id=1, source_target_pairs={{0,2},{1,3},{2,0},{3,1},{4,6},{5,7},{6,4},{7,5}} | collective-permute-start | bytes 786440 | tf_op jit(solution)/shard_map/ppermute | solution.py:341
  380.8 39.6 %collective-permute-start.40 = (f32[128,512]{1,0:T(8,128)}, f32[128,512]{1,0:T(8,128)S(1)}, u32[]{:S(2)}, u32[]{:S(2)}) collective-permute-start(f32[128,512]{1,0:T(8,128)} %get-tuple-element.212.refs_2_), channel_id=1, source_target_pairs={{0,1},{1,0},{2,3},{3,2},{4,5},{5,4},{6,7},{7,6}} | collective-permute-start | bytes 786440 | tf_op jit(solution)/shard_map/ppermute | solution.py:341
  414.1 63.1 %collective-permute-start.49 = (f32[640,512]{1,0:T(8,128)S(1)}, f32[640,512]{1,0:T(8,128)}, u32[]{:S(2)}, u32[]{:S(2)}) collective-permute-start(f32[640,512]{1,0:T(8,128)S(1)} %copy-done.4), channel_id=1, source_target_pairs={{0,1},{1,0},{2,3},{3,2},{4,5},{5,4},{6,7},{7,6}} | collective-permute-start | bytes 3932168 | tf_op jit(solution)/shard_map/ppermute | solution.py:341
  494.5 65.7 %collective-permute-start.55 = (f32[512,512]{1,0:T(8,128)S(1)}, f32[512,512]{1,0:T(8,128)S(1)}, u32[]{:S(2)}, u32[]{:S(2)}) collective-permute-start(f32[512,512]{1,0:T(8,128)S(1)} %copy-done.7), channel_id=1, source_target_pairs={{0,2},{1,3},{2,0},{3,1},{4,6},{5,7},{6,4},{7,5}} | collective-permute-start | bytes 3145736 | tf_op jit(solution)/shard_map/ppermute | solution.py:341
  495.3 64.9 %collective-permute-start.54 = (f32[896,256]{1,0:T(8,128)}, f32[896,256]{1,0:T(8,128)}, u32[]{:S(2)}, u32[]{:S(2)}) collective-permute-start(f32[896,256]{1,0:T(8,128)} %get-tuple-element.232), channel_id=1, source_target_pairs={{0,4},{4,0},{1,5},{5,1},{2,6},{6,2},{3,7},{7,3}} | collective-permute-start | bytes 2752520 | tf_op jit(solution)/shard_map/ppermute | solution.py:347
  497.3 33.6 %collective-permute-start.52 = (f32[128,512]{1,0:T(8,128)}, f32[128,512]{1,0:T(8,128)S(1)}, u32[]{:S(2)}, u32[]{:S(2)}) collective-permute-start(f32[128,512]{1,0:T(8,128)} %get-tuple-element.230.refs_2_), channel_id=1, source_target_pairs={{0,2},{1,3},{2,0},{3,1},{4,6},{5,7},{6,4},{7,5}} | collective-permute-start | bytes 786440 | tf_op jit(solution)/shard_map/ppermute | solution.py:341
  498.2 33.4 %collective-permute-start.51 = (f32[128,512]{1,0:T(8,128)}, f32[128,512]{1,0:T(8,128)S(1)}, u32[]{:S(2)}, u32[]{:S(2)}) collective-permute-start(f32[128,512]{1,0:T(8,128)} %get-tuple-element.230.refs_2_), channel_id=1, source_target_pairs={{0,1},{1,0},{2,3},{3,2},{4,5},{5,4},{6,7},{7,6}} | collective-permute-start | bytes 786440 | tf_op jit(solution)/shard_map/ppermute | solution.py:341
  524.6 37.8 %collective-permute-start.59 = (f32[4,128,256]{2,1,0:T(8,128)}, f32[4,128,256]{2,1,0:T(8,128)}, u32[]{:S(2)}, u32[]{:S(2)}) collective-permute-start(f32[4,128,256]{2,1,0:T(8,128)} %slice_select_fusion.4), channel_id=1, source_target_pairs={{0,4},{4,0},{1,5},{5,1},{2,6},{6,2},{3,7},{7,3}} | collective-permute-start | bytes 1572872 | tf_op jit(solution)/shard_map/ppermute | solution.py:347
  530.9 55.0 %collective-permute-start.60 = (f32[512,512]{1,0:T(8,128)S(1)}, f32[512,512]{1,0:T(8,128)S(1)}, u32[]{:S(2)}, u32[]{:S(2)}) collective-permute-start(f32[512,512]{1,0:T(8,128)S(1)} %copy-done.7), channel_id=1, source_target_pairs={{0,1},{1,0},{2,3},{3,2},{4,5},{5,4},{6,7},{7,6}} | collective-permute-start | bytes 3145736 | tf_op jit(solution)/shard_map/ppermute | solution.py:341
  574.0 88.2 %collective-permute-start.65 = (f32[768,256]{1,0:T(8,128)}, f32[768,256]{1,0:T(8,128)}, u32[]{:S(2)}, u32[]{:S(2)}) collective-permute-start(f32[768,256]{1,0:T(8,128)} %get-tuple-element.250), channel_id=1, source_target_pairs={{0,4},{4,0},{1,5},{5,1},{2,6},{6,2},{3,7},{7,3}} | collective-permute-start | bytes 2359304 | tf_op jit(solution)/shard_map/ppermute | solution.py:347
  603.5 58.7 %collective-permute-start.66 = (f32[384,512]{1,0:T(8,128)S(1)}, f32[384,512]{1,0:T(8,128)S(1)}, u32[]{:S(2)}, u32[]{:S(2)}) collective-permute-start(f32[384,512]{1,0:T(8,128)S(1)} %copy-done.11), channel_id=1, source_target_pairs={{0,2},{1,3},{2,0},{3,1},{4,6},{5,7},{6,4},{7,5}} | collective-permute-start | bytes 2359304 | tf_op jit(solution)/shard_map/ppermute | solution.py:341
  628.0 36.5 %collective-permute-start.70 = (f32[3,128,256]{2,1,0:T(8,128)}, f32[3,128,256]{2,1,0:T(8,128)S(1)}, u32[]{:S(2)}, u32[]{:S(2)}) collective-permute-start(f32[3,128,256]{2,1,0:T(8,128)} %slice_select_fusion.17), channel_id=1, source_target_pairs={{0,4},{4,0},{1,5},{5,1},{2,6},{6,2},{3,7},{7,3}} | collective-permute-start | bytes 1179656 | tf_op jit(solution)/shard_map/ppermute | solution.py:347
  633.8 54.6 %collective-permute-start.71 = (f32[384,512]{1,0:T(8,128)S(1)}, f32[384,512]{1,0:T(8,128)S(1)}, u32[]{:S(2)}, u32[]{:S(2)}) collective-permute-start(f32[384,512]{1,0:T(8,128)S(1)} %copy-done.11), channel_id=1, source_target_pairs={{0,1},{1,0},{2,3},{3,2},{4,5},{5,4},{6,7},{7,6}} | collective-permute-start | bytes 2359304 | tf_op jit(solution)/shard_map/ppermute | solution.py:341
  676.8 78.1 %collective-permute-start.76 = (f32[640,256]{1,0:T(8,128)}, f32[640,256]{1,0:T(8,128)}, u32[]{:S(2)}, u32[]{:S(2)}) collective-permute-start(f32[640,256]{1,0:T(8,128)} %get-tuple-element.268), channel_id=1, source_target_pairs={{0,4},{4,0},{1,5},{5,1},{2,6},{6,2},{3,7},{7,3}} | collective-permute-start | bytes 1966088 | tf_op jit(solution)/shard_map/ppermute | solution.py:347
  706.9 49.3 %collective-permute-start.77 = (f32[256,512]{1,0:T(8,128)}, f32[256,512]{1,0:T(8,128)S(1)}, u32[]{:S(2)}, u32[]{:S(2)}) collective-permute-start(f32[256,512]{1,0:T(8,128)} %get-tuple-element.271.refs_31_.refs_32_), channel_id=1, source_target_pairs={{0,2},{1,3},{2,0},{3,1},{4,6},{5,7},{6,4},{7,5}} | collective-permute-start | bytes 1572872 | tf_op jit(solution)/shard_map/ppermute | solution.py:341
  713.8 42.5 %collective-permute-start.81 = (f32[2,128,256]{2,1,0:T(8,128)S(1)}, f32[2,128,256]{2,1,0:T(8,128)S(1)}, u32[]{:S(2)}, u32[]{:S(2)}) collective-permute-start(f32[2,128,256]{2,1,0:T(8,128)S(1)} %slice_select_fusion.18), channel_id=1, source_target_pairs={{0,4},{4,0},{1,5},{5,1},{2,6},{6,2},{3,7},{7,3}} | collective-permute-start | bytes 786440 | tf_op jit(solution)/shard_map/ppermute | solution.py:347
  726.4 30.7 %collective-permute-start.80 = (f32[256,512]{1,0:T(8,128)}, f32[256,512]{1,0:T(8,128)S(1)}, u32[]{:S(2)}, u32[]{:S(2)}) collective-permute-start(f32[256,512]{1,0:T(8,128)} %get-tuple-element.275.refs_35_.refs_3_), channel_id=1, source_target_pairs={{0,3},{1,2},{2,1},{3,0},{4,7},{5,6},{6,5},{7,4}} | collective-permute-start | bytes 1572872 | tf_op jit(solution)/shard_map/ppermute | solution.py:341
  756.7 38.6 %collective-permute-start.87 = (f32[512,256]{1,0:T(8,128)}, f32[512,256]{1,0:T(8,128)}, u32[]{:S(2)}, u32[]{:S(2)}) collective-permute-start(f32[512,256]{1,0:T(8,128)} %get-tuple-element.286), channel_id=1, source_target_pairs={{0,4},{4,0},{1,5},{5,1},{2,6},{6,2},{3,7},{7,3}} | collective-permute-start | bytes 1572872 | tf_op jit(solution)/shard_map/ppermute | solution.py:347
  794.8 34.9 %collective-permute-start.91 = (f32[256,512]{1,0:T(8,128)}, f32[256,512]{1,0:T(8,128)S(1)}, u32[]{:S(2)}, u32[]{:S(2)}) collective-permute-start(f32[256,512]{1,0:T(8,128)} %get-tuple-element.293.refs_3_.refs_40_), channel_id=1, source_target_pairs={{0,3},{1,2},{2,1},{3,0},{4,7},{5,6},{6,5},{7,4}} | collective-permute-start | bytes 1572872 | tf_op jit(solution)/shard_map/ppermute | solution.py:341
  795.3 34.3 %collective-permute-start.90 = (f32[256,512]{1,0:T(8,128)}, f32[256,512]{1,0:T(8,128)S(1)}, u32[]{:S(2)}, u32[]{:S(2)}) collective-permute-start(f32[256,512]{1,0:T(8,128)} %get-tuple-element.293.refs_3_.refs_40_), channel_id=1, source_target_pairs={{0,2},{1,3},{2,0},{3,1},{4,6},{5,7},{6,4},{7,5}} | collective-permute-start | bytes 1572872 | tf_op jit(solution)/shard_map/ppermute | solution.py:341
  796.4 33.3 %collective-permute-start.89 = (f32[256,512]{1,0:T(8,128)}, f32[256,512]{1,0:T(8,128)S(1)}, u32[]{:S(2)}, u32[]{:S(2)}) collective-permute-start(f32[256,512]{1,0:T(8,128)} %get-tuple-element.293.refs_3_.refs_40_), channel_id=1, source_target_pairs={{0,1},{1,0},{2,3},{3,2},{4,5},{5,4},{6,7},{7,6}} | collective-permute-start | bytes 1572872 | tf_op jit(solution)/shard_map/ppermute | solution.py:341
  848.0 41.1 %collective-permute-start.98 = (f32[384,256]{1,0:T(8,128)S(1)}, f32[384,256]{1,0:T(8,128)S(1)}, u32[]{:S(2)}, u32[]{:S(2)}) collective-permute-start(f32[384,256]{1,0:T(8,128)S(1)} %copy-done.63), channel_id=1, source_target_pairs={{0,4},{4,0},{1,5},{5,1},{2,6},{6,2},{3,7},{7,3}} | collective-permute-start | bytes 1179656 | tf_op jit(solution)/shard_map/ppermute | solution.py:347
  856.8 35.8 %collective-permute-start.99 = (f32[256,256]{1,0:T(8,128)}, f32[256,256]{1,0:T(8,128)S(1)}, u32[]{:S(2)}, u32[]{:S(2)}) collective-permute-start(f32[256,256]{1,0:T(8,128)} %get-tuple-element.311), channel_id=1, source_target_pairs={{0,4},{4,0},{1,5},{5,1},{2,6},{6,2},{3,7},{7,3}} | collective-permute-start | bytes 786440 | tf_op jit(solution)/shard_map/ppermute | solution.py:347
  (140 other events, 1488.0 us)
